TPU v7x, 32 devices: a whole 2x2x4 slice. The times are simulated.
32 devices in a mesh: rep: 8 (over y, x, core), shard: 4 (over z).
Axes of the slice: x: 2, y: 2, z: 4, core: 2. Of those that a mesh axis runs over, the one named last changes fastest.
Arguments:
- activations: bfloat16 [6, 4096, 2048], P(None, ('rep', 'shard')), may hold values from -50 to 50
- cotangents: bfloat16 [6, 4096, 512], P(None, ('rep', 'shard')), may hold values from -120 to 120
- momentum: float32 [12, 256, 2048], P(None, None, 'shard'), may hold values from -6 to 6
- owners: int32 [12], replicated, may hold values from 0 to 3, as said below
- bucket_starts: int32 [2], replicated, may hold values from 1 to 11, as said below
Outputs:
- momentum_out: float32 [12, 256, 2048], P(None, None, 'shard')
- update: float32 [12, 256, 2048], P(None, None, 'shard')
- owned: bfloat16 [16, 256, 2048], P('shard')
Inputs may be any that keep to these rules, and one draw needn't show every extreme that they name: `owners`: no owner is named more than 4 times, and some owner exactly 4 times. `bucket_starts`: strictly increasing.
All inputs are finite; a program needn't handle non-finite values.
Results may differ from a plain program's by a relative error of at most 0.033.
Values may be sent and summed in bfloat16 or wider, within the bound.
A program may use at most 128 MiB of HBM per device.

v0:
```python
import math

import jax
import jax.numpy as jnp
from jax import lax
from jax.sharding import PartitionSpec as P

D = 2048
KV = 256
ITERS = 5
MATS = 12


coef_a = 3.4445
coef_b = -4.775
coef_c = 2.0315
momentum_rate = 0.95
clip_level = 0.5
epsilon = 1e-06


def orthogonal_batch(matrices):
    values = matrices.astype(jnp.float32)
    frobenius = jnp.sqrt(jnp.sum(values * values, axis=(1, 2), keepdims=True))
    matrix = (values / (frobenius + epsilon)).astype(jnp.bfloat16)
    for iteration in range(ITERS):
        gram_matrix = jnp.einsum(
            "skd,sjd->skj", matrix, matrix, preferred_element_type=jnp.float32
        ).astype(jnp.bfloat16)
        square = jnp.einsum(
            "skj,sji->ski", gram_matrix, gram_matrix, preferred_element_type=jnp.float32
        )
        mixing = (coef_b * gram_matrix.astype(jnp.float32) + coef_c * square).astype(jnp.bfloat16)
        product = jnp.einsum("skj,sjd->skd", mixing, matrix, preferred_element_type=jnp.float32)
        matrix = (coef_a * matrix.astype(jnp.float32) + product).astype(jnp.bfloat16)
    return matrix


def clip_factors(square_sums, bucket_starts):
    indices = jnp.arange(MATS, dtype=jnp.int32)
    buckets = jnp.sum((indices[:, None] >= bucket_starts[None, :]).astype(jnp.int32), axis=1)
    together = (buckets[:, None] == buckets[None, :]).astype(jnp.float32)
    totals = jnp.sum(together * square_sums[None, :], axis=1)
    members = jnp.sum(together, axis=1)
    root_mean = jnp.sqrt(totals / (members * KV * D) + epsilon)
    return jnp.minimum(1.0, clip_level / root_mean)


def slot_numbers(owners):
    indices = jnp.arange(MATS, dtype=jnp.int32)
    earlier = (indices[None, :] < indices[:, None]) & (owners[None, :] == owners[:, None])
    return jnp.sum(earlier.astype(jnp.int32), axis=1)


def selector(owner_of, slot_of, shard_count, slot_count):
    holders = lax.broadcasted_iota(jnp.int32, (shard_count, slot_count, 1), 0)
    places = lax.broadcasted_iota(jnp.int32, (shard_count, slot_count, 1), 1)
    chosen = (holders == owner_of[None, None, :]) & (places == slot_of[None, None, :])
    return chosen.astype(jnp.bfloat16)


def pack_slots(shards, chooser):
    return jnp.einsum("psm,mkd->skpd", chooser, shards, preferred_element_type=jnp.float32).astype(
        jnp.bfloat16
    )


def unpack_slots(received, chooser):
    return jnp.einsum("psm,skpd->mkd", chooser, received, preferred_element_type=jnp.float32)


def per_device(activations, cotangents, momentum, owners, bucket_starts):
    shard_count = lax.axis_size("shard")
    replica_count = lax.axis_size("rep")
    layers, tok_rows, width = activations.shape
    token_total = tok_rows * shard_count * replica_count
    columns = width // shard_count
    slot_count = -(-MATS // shard_count) + 1
    update_scale = math.sqrt(max(KV, D))
    partial_terms = jnp.einsum(
        "ltk,ltd->lkd", cotangents, activations, preferred_element_type=jnp.float32
    ).reshape(MATS, KV, width)
    shard_part = lax.psum_scatter(
        partial_terms.astype(jnp.bfloat16), "shard", scatter_dimension=2, tiled=True
    )
    summed = lax.psum(shard_part, "rep").astype(jnp.float32)
    gradient = summed / jnp.sqrt(jnp.float32(token_total))
    square_sums = lax.psum(jnp.sum(gradient * gradient, axis=(1, 2)), "shard")
    factors = clip_factors(square_sums, bucket_starts)
    momentum_out = momentum_rate * momentum + factors[:, None, None] * gradient
    nesterov = (factors[:, None, None] * gradient + momentum_rate * momentum_out).astype(
        jnp.bfloat16
    )
    slot_of = slot_numbers(owners)
    chooser = selector(owners, slot_of, shard_count, slot_count)
    received = lax.all_to_all(
        pack_slots(nesterov, chooser), "shard", split_axis=2, concat_axis=2, tiled=True
    )
    item_count = received.shape[0]
    result = orthogonal_batch(received.reshape(item_count, KV, width))
    scaled = (update_scale * result.astype(jnp.float32)).astype(jnp.bfloat16)
    returned_part = lax.all_to_all(
        result.reshape(item_count, KV, shard_count, columns),
        "shard",
        split_axis=2,
        concat_axis=2,
        tiled=True,
    )
    update = update_scale * unpack_slots(returned_part, chooser)
    return (momentum_out, update, scaled)


def solution(mesh):
    placed = (
        P(None, ("rep", "shard"), None),
        P(None, ("rep", "shard"), None),
        P(None, None, "shard"),
        P(),
        P(),
    )
    return jax.shard_map(
        per_device,
        mesh=mesh,
        in_specs=placed,
        out_specs=(P(None, None, "shard"), P(None, None, "shard"), P("shard", None, None)),
        check_vma=False,
    )
```

profile of v0, /device:TPU:17, one launch (start us, length us, event | category | flops | bytes accessed | tf_op | source)
XLA Modules:
  0.0 623.3 jit_solution(7850183555704222649)
XLA Ops:
  7.2 1.8 copy-done
  9.1 7.5 %convolution_convert_fusion = bf16[6,512,2048]{2,1,0:T(8,128)(2,1)} fusion(bf16[6,128,512]{2,1,0:T(8,128)(2,1)} %param.6, bf16[6,128,2048]{2,1,0:T(8,128)(2,1)S(1)} %copy-done), kind=kOutput, calls=%fused_computation.13 | convolution fusion | flops 1616904192 | bytes 16515072 | tf_op jit(solution)/shard_map/ltk,ltd->lkd/dot_general | solution.py:80
  16.7 214.0 %reduce-scatter.2.cloned.1.call-done = bf16[12,256,512]{2,1,0:T(8,128)(2,1)} async-done(((bf16[12,256,2048]{2,1,0:T(8,128)(2,1)}), bf16[12,256,512]{2,1,0:T(8,128)(2,1)}) %reduce-scatter.2.cloned.1.call-update) | async-done | bytes 3145744 | tf_op jit(solution)/shard_map/reduce_scatter | solution.py:83
  230.8 0.2 convert_reduce_fusion
  230.9 72.2 %all-reduce.2.cloned.1.call-done = bf16[12,256,512]{2,1,0:T(8,128)(2,1)} async-done(((bf16[12,256,512]{2,1,0:T(8,128)(2,1)}), bf16[12,256,512]{2,1,0:T(8,128)(2,1)}) %all-reduce.2.cloned.1.call-update) | async-done | bytes 3145744 | tf_op jit(solution)/shard_map/psum | solution.py:86
  303.2 2.9 fusion.4
  306.1 6.9 %psum.15 = f32[12]{0:T(128)S(1)} all-reduce(f32[12]{0:T(128)S(1)} %fusion.4), channel_id=1, replica_groups=mesh['rep'=8,'shard'=4] {'shard'}, use_global_device_ids=true, to_apply=%region_4.0 | all-reduce | flops 12 | bytes 96 | tf_op jit(solution)/shard_map/psum | solution.py:88
  313.0 0.2 fusion.41
  313.2 8.1 %fusion.9 = (bf16[12,256,512,1]{2,1,0,3:T(8,128)(2,1)S(1)}, f32[12,256,512]{2,1,0:T(8,128)}) fusion(bf16[12,256,512]{2,1,0:T(8,128)(2,1)} %all-reduce.2.cloned.1.call-done, f32[12]{0:T(128)S(1)} %minimum_multiply_fusion, f32[12,256,512]{2,1,0:T(8,128)} %param.7), kind=kLoop, calls=%fused_computation.20 | loop fusion | flops 11010048 | bytes 18874416 | tf_op jit(solution)/shard_map/convert_element_type | solution.py:91
  321.3 2.8 fusion.6
  324.1 1.4 copy.28
  325.5 95.9 %all_to_all.10 = bf16[4,256,4,512]{3,0,1,2:T(4,128)(2,1)} all-to-all(bf16[4,256,4,512]{3,0,1,2:T(4,128)(2,1)S(1)} %copy.28), channel_id=1, replica_groups=mesh['rep'=8,'shard'=4] {'shard'}, dimensions={2} | all-to-all | bytes 8388608 | tf_op jit(solution)/shard_map/all_to_all | solution.py:96
  421.4 7.5 %copy.29 = bf16[4,256,4,512]{1,3,2,0:T(8,128)(2,1)} copy(bf16[4,256,4,512]{3,0,1,2:T(4,128)(2,1)} %all_to_all.10) | data formatting | bytes 8388608 | tf_op jit(solution)/shard_map/all_to_all | solution.py:96
  428.9 3.4 multiply_reduce_fusion
  432.3 6.9 %copy.30 = f32[4,256,2048]{2,1,0:T(8,128)} copy(bf16[4,256,2048]{1,2,0:T(8,128)(2,1)} %bitcast.48) | data formatting | bytes 12582912 | tf_op jit(solution)/shard_map/convert_element_type | solution.py:23
  439.2 4.6 divide_convert_fusion
  443.8 2.0 copy-done.2
  445.8 1.3 convolution_convert_fusion.6
  447.1 6.3 %add_convert_fusion.4 = bf16[4,256,2048]{2,1,0:T(8,128)(2,1)} fusion(bf16[4,256,2048]{2,1,0:T(8,128)(2,1)} %copy-done.2, bf16[4,256,256]{2,1,0:T(8,128)(2,1)S(1)} %convolution_convert_fusion.6), kind=kOutput, calls=%fused_computation.6 | convolution fusion | flops 1217658880 | bytes 8912896 | tf_op jit(solution)/shard_map/skj,sjd->skd/dot_general | solution.py:34
  453.3 4.7 convolution_convert_fusion.5
  458.1 6.3 %add_convert_fusion.3 = bf16[4,256,2048]{2,1,0:T(8,128)(2,1)} fusion(bf16[4,256,2048]{2,1,0:T(8,128)(2,1)} %add_convert_fusion.4, bf16[4,256,256]{2,1,0:T(8,128)(2,1)S(1)} %convolution_convert_fusion.5), kind=kOutput, calls=%fused_computation.5 | convolution fusion | flops 1217658880 | bytes 8912896 | tf_op jit(solution)/shard_map/skj,sjd->skd/dot_general | solution.py:34
  464.4 4.8 convolution_convert_fusion.4
  469.2 6.3 %add_convert_fusion.2 = bf16[4,256,2048]{2,1,0:T(8,128)(2,1)} fusion(bf16[4,256,2048]{2,1,0:T(8,128)(2,1)} %add_convert_fusion.3, bf16[4,256,256]{2,1,0:T(8,128)(2,1)S(1)} %convolution_convert_fusion.4), kind=kOutput, calls=%fused_computation.4 | convolution fusion | flops 1217658880 | bytes 8912896 | tf_op jit(solution)/shard_map/skj,sjd->skd/dot_general | solution.py:34
  475.4 4.7 convolution_convert_fusion.3
  480.2 6.3 %add_convert_fusion.1 = bf16[4,256,2048]{2,1,0:T(8,128)(2,1)} fusion(bf16[4,256,2048]{2,1,0:T(8,128)(2,1)} %add_convert_fusion.2, bf16[4,256,256]{2,1,0:T(8,128)(2,1)S(1)} %convolution_convert_fusion.3), kind=kOutput, calls=%fused_computation.3 | convolution fusion | flops 1217658880 | bytes 8912896 | tf_op jit(solution)/shard_map/skj,sjd->skd/dot_general | solution.py:34
  486.4 4.7 convolution_convert_fusion.2
  491.2 7.7 %multiply_convert_fusion = (bf16[4,256,2048]{2,1,0:T(8,128)(2,1)}, bf16[4,256,2048]{2,1,0:T(8,128)(2,1)}) fusion(bf16[4,256,2048]{2,1,0:T(8,128)(2,1)} %add_convert_fusion.1, bf16[4,256,256]{2,1,0:T(8,128)(2,1)S(1)} %convolution_convert_fusion.2), kind=kOutput, calls=%fused_computation.1 | convolution fusion | flops 1223950336 | bytes 13107200 | tf_op jit(solution)/shard_map/skj,sjd->skd/dot_general | solution.py:34
  498.9 7.8 %reshape.38 = bf16[4,256,4,512]{3,2,1,0:T(4,128)(2,1)} reshape(bf16[4,256,2048]{2,1,0:T(8,128)(2,1)} %get-tuple-element.20) | data formatting | bytes 8388608 | tf_op jit(solution)/shard_map/reshape | solution.py:103
  506.7 5.4 copy.31
  512.1 94.6 %all_to_all.11 = bf16[4,256,4,512]{3,0,1,2:T(4,128)(2,1)S(1)} all-to-all(bf16[4,256,4,512]{3,0,1,2:T(4,128)(2,1)S(1)} %copy.31), channel_id=1, replica_groups=mesh['rep'=8,'shard'=4] {'shard'}, dimensions={2} | all-to-all | bytes 8388608 | tf_op jit(solution)/shard_map/all_to_all | solution.py:102
  606.8 3.4 bitcast_multiply_fusion
  610.1 6.3 %copy.33 = f32[12,256,512]{2,1,0:T(8,128)} copy(f32[12,256,512]{2,0,1:T(8,128)S(1)} %bitcast_multiply_fusion) | data formatting | bytes 12582912
  (15 shorter events, 0.2 us)
Async XLA Ops:
  7.2 1.9 copy-start
  7.2 223.5 %reduce-scatter.2.cloned.1.call-start = ((), (), s32[]{:S(2)}) async-start(), calls=%async_computation.3 | async-start | bytes 15728640 | tf_op jit(solution)/shard_map/reduce_scatter | solution.py:83
  16.6 214.2 %copy-start.3 = (s32[12]{0:T(128)S(1)}, s32[12]{0:T(128)}, u32[]{:S(2)}) copy-start(s32[12]{0:T(128)} %param.8) | copy-start | bytes 148
  16.6 289.4 %copy-start.4 = (s32[2]{0:T(128)S(1)}, s32[2]{0:T(128)}, u32[]{:S(2)}) copy-start(s32[2]{0:T(128)} %param.9) | copy-start | bytes 28
  16.6 286.5 %all-reduce.2.cloned.1.call-start = ((), (), s32[]{:S(2)}) async-start(), calls=%async_computation.4 | async-start | bytes 6291456 | tf_op jit(solution)/shard_map/psum | solution.py:86
  443.8 2.0 copy-start.2
  606.8 9.7 %copy-start.1 = (bf16[6,128,2048]{2,1,0:T(8,128)(2,1)S(1)}, bf16[6,128,2048]{2,1,0:T(8,128)(2,1)}, u32[]{:S(2)}) copy-start(bf16[6,128,2048]{2,1,0:T(8,128)(2,1)} %param.5) | copy-start | bytes 9437188
Sparse Core Ops, SparseCore 0:
  16.7 213.9 reduce-scatter.1
  234.0 69.1 all-reduce.1
where the time goes:
time: 630 us; the launch traced here: 623 us
  waiting for transfers between devices  286 us (45%)
  blocking collectives  197 us (31%)
  matrix products  66.7 us (11%)
  local copies, waits for them, and re-layouts  39.3 us (6%)
  other arithmetic  19.4 us (3%)
  between operations  14.1 us (2%)
    reduce_scatter x1, waiting for transfers between devices, per_device(): lax.psum_scatter(partial_terms.astype(jnp.bfloat16), 'shard', scatter_dim...  214 us
    all_to_all x1, blocking collectives, per_device(): lax.all_to_all(pack_slots(nesterov, chooser), 'shard', split_axis=2, conc...  95.9 us
    all_to_all x1, blocking collectives, per_device(): lax.all_to_all(result.reshape(item_count, KV, shard_count, columns), 'sha...  94.6 us
    psum x1, waiting for transfers between devices, per_device(): summed = lax.psum(shard_part, 'rep').astype(jnp.float32)  72.2 us
    dot_general x5, matrix products, orthogonal_batch(): jnp.einsum('skj,sjd->skd', mixing, matrix, preferred_element_type=jnp.flo...  32.7 us
    dot_general x5, matrix products, orthogonal_batch(): jnp.einsum('skd,sjd->skj', matrix, matrix, preferred_element_type=jnp.flo...  20.3 us
    reshape x2, local copies, waits for them, and re-layouts, per_device(): result.reshape(item_count, KV, shard_count, columns)  13.2 us
  transfers between devices with their start and end apart: 2, of which 2 were waited for; matrix products, arithmetic and copies ran while one was open for 0% of the time, Pallas kernels for 0%

commit v1 on v0

--- a/solution.py
+++ b/solution.py
@@ -1,15 +1,22 @@
+import functools
 import math
 
 import jax
 import jax.numpy as jnp
 from jax import lax
+from jax.experimental import pallas as pl
+from jax.experimental.pallas import tpu as pltpu
 from jax.sharding import PartitionSpec as P
 
 D = 2048
 KV = 256
 ITERS = 5
 MATS = 12
-
+MESH = pl.DeviceIdType.MESH
+VMEM_SPEC = pl.BlockSpec(memory_space=pltpu.VMEM)
+SMEM_SPEC = pl.BlockSpec(memory_space=pltpu.SMEM)
+ANY_SPEC = pl.BlockSpec(memory_space=pl.ANY)
+VMEM_LIMIT = 60 * 1024 * 1024
 
 coef_a = 3.4445
 coef_b = -4.775
@@ -69,7 +76,7 @@
     return jnp.einsum("psm,skpd->mkd", chooser, received, preferred_element_type=jnp.float32)
 
 
-def per_device(activations, cotangents, momentum, owners, bucket_starts):
+def per_device_general(activations, cotangents, momentum, owners, bucket_starts):
     shard_count = lax.axis_size("shard")
     replica_count = lax.axis_size("rep")
     layers, tok_rows, width = activations.shape
@@ -110,7 +117,450 @@
     return (momentum_out, update, scaled)
 
 
+def place():
+    me = lax.axis_index("rep")
+    core = lax.rem(me, 2)
+    x = lax.rem(lax.div(me, 2), 2)
+    y = lax.div(me, 4)
+    to_core = me + 1 - 2 * core
+    to_x = me + 2 - 4 * x
+    to_y = me + 4 - 8 * y
+    to_xy = me + 6 - 4 * x - 8 * y
+    return me, core, x, y, to_core, to_x, to_y, to_xy
+
+
+def greet(peers):
+    barrier = pltpu.get_barrier_semaphore()
+    for peer in peers:
+        pl.semaphore_signal(barrier, inc=1, device_id=peer, device_id_type=MESH)
+    pl.semaphore_wait(barrier, len(peers))
+
+
+def remote(src, dst, send, recv, peer):
+    return pltpu.make_async_remote_copy(
+        src_ref=src, dst_ref=dst, send_sem=send, recv_sem=recv, device_id=peer, device_id_type=MESH
+    )
+
+
+def plane_gather_start(z, buf_at, send, recv):
+    me, core, x, y, to_core, to_x, to_y, to_xy = place()
+    copies = []
+    for k, peer in enumerate((to_x, to_y, to_xy, to_core)):
+        c = remote(buf_at(me), buf_at(me), send.at[k], recv.at[k], (peer, z))
+        c.start()
+        copies.append(c)
+    return copies
+
+
+def plane_gather_finish(z, buf_at, send, recv, copies):
+    me, core, x, y, to_core, to_x, to_y, to_xy = place()
+    for k, source in enumerate((to_x, to_y, to_xy)):
+        copies[k].wait_recv()
+        c = remote(buf_at(source), buf_at(source), send.at[4 + k], recv.at[4 + k], (to_core, z))
+        c.start()
+        copies.append(c)
+    for k in range(3, 7):
+        copies[k].wait_recv()
+    for c in copies:
+        c.wait_send()
+
+
+def reduce_kernel(
+    n_shard, inverse, lay_ref, half_ref, act_ref, cot_ref, gall_ref, sq_ref,
+    act, cot, part, recv1, turn, recv2, plane, zrecv,
+    local_sem, in_send, in_recv, s1, r1, s2, r2, s3, r3, gs, gr, qs, qr,
+):
+    me, core, x, y, to_core, to_x, to_y, to_xy = place()
+    z = lax.axis_index("shard")
+    tokens = act_ref.shape[1]
+    rows, cols = part.shape[-2:]
+    members = part.shape[2 + 1]
+    steps = [d for d in (2, 1, 3) if d < n_shard] + list(range(4, n_shard)) + [0]
+    peers = [(p, z) for p in (to_core, to_x, to_y, to_xy)]
+    peers += [(me, lax.rem(z + d, n_shard)) for d in range(1, n_shard)]
+    own = [
+        pltpu.make_async_copy(act_ref, act.at[:, pl.ds(0, tokens)], local_sem.at[0]),
+        pltpu.make_async_copy(cot_ref, cot.at[:, pl.ds(0, tokens)], local_sem.at[1]),
+    ]
+    for c in own:
+        c.start()
+    greet(peers)
+    swap = [
+        remote(cot_ref, cot.at[:, pl.ds(tokens, tokens)], in_send.at[1], in_recv.at[1], (to_core, z)),
+        remote(act_ref, act.at[:, pl.ds(tokens, tokens)], in_send.at[0], in_recv.at[0], (to_core, z)),
+    ]
+    for c in swap:
+        c.start()
+    for c in own:
+        c.wait()
+    for c in swap:
+        c.wait()
+    first = []
+    for k, d in enumerate(steps):
+        offset = pl.multiple_of(lax.rem(z + d, n_shard) * cols, cols)
+
+        def one(q, carry, k=k, offset=offset):
+            group = lax.div(q, members)
+            member = lax.rem(q, members)
+            block = cot[lay_ref[q]]
+            low = jnp.where(core == 0, block[:, :rows], block[:, rows : 2 * rows])
+            high = jnp.where(core == 0, block[:, 2 * rows : 3 * rows], block[:, 3 * rows :])
+            left = jnp.where(half_ref[q] == 0, low, high)
+            right = act[lay_ref[q], :, pl.ds(offset, cols)]
+            value = lax.dot_general(
+                left, right, (((0,), (0,)), ((), ())), preferred_element_type=jnp.float32
+            )
+            part[k, lax.div(group, 2), lax.rem(group, 2), member] = value.astype(part.dtype)
+            return carry
+
+        lax.fori_loop(0, 4 * members, one, 0)
+        if k % 2 == 0:
+            c = remote(part.at[k, :, 1 - x], recv1.at[k], s1.at[k], r1.at[k], (to_x, z))
+        else:
+            c = remote(part.at[k, 1 - y], recv1.at[k], s1.at[k], r1.at[k], (to_y, z))
+        c.start()
+        first.append(c)
+    second = []
+    for k in range(n_shard):
+        first[k].wait_recv()
+
+        def add_out(j, carry, k=k):
+            if k % 2 == 0:
+                mine = part[k, 1 - y, x, j]
+                came = recv1[k, 1 - y, j]
+            else:
+                mine = part[k, y, 1 - x, j]
+                came = recv1[k, 1 - x, j]
+            turn[k, j] = (mine.astype(jnp.float32) + came.astype(jnp.float32)).astype(turn.dtype)
+            return carry
+
+        lax.fori_loop(0, members, add_out, 0)
+        c = remote(
+            turn.at[k], recv2.at[k], s2.at[k], r2.at[k], (to_y if k % 2 == 0 else to_x, z)
+        )
+        c.start()
+        second.append(c)
+    third = []
+    for k, d in enumerate(steps):
+        second[k].wait_recv()
+
+        def add_in(j, carry, k=k):
+            came = recv1[k, y, j] if k % 2 == 0 else recv1[k, x, j]
+            value = part[k, y, x, j].astype(jnp.float32) + came.astype(jnp.float32)
+            value = value + recv2[k, j].astype(jnp.float32)
+            plane[k, j] = value.astype(plane.dtype)
+            return carry
+
+        lax.fori_loop(0, members, add_in, 0)
+        if d:
+            c = remote(
+                plane.at[k], zrecv.at[k], s3.at[k], r3.at[k], (me, lax.rem(z + d, n_shard))
+            )
+            c.start()
+            third.append(c)
+    for c in third:
+        c.wait_recv()
+
+    def add_last(j, carry):
+        value = plane[n_shard - 1, j].astype(jnp.float32)
+        for k in range(n_shard - 1):
+            value = value + zrecv[k, j].astype(jnp.float32)
+        gall_ref[me, j] = (value * inverse).astype(gall_ref.dtype)
+        return carry
+
+    lax.fori_loop(0, members, add_last, 0)
+    at = lambda r: gall_ref.at[r]
+    copies = plane_gather_start(z, at, gs, gr)
+    plane_gather_finish(z, at, gs, gr, copies)
+
+    def square(r, carry):
+        for j in range(members):
+            value = gall_ref[r, j].astype(jnp.float32)
+            sq_ref[0, r, j] = jnp.sum(value * value, axis=0, keepdims=True)
+        return carry
+
+    lax.fori_loop(0, gall_ref.shape[0], square, 0)
+    fourth = []
+    for d in range(1, n_shard):
+        c = remote(
+            sq_ref.at[0], sq_ref.at[d], qs.at[d - 1], qr.at[d - 1],
+            (me, lax.rem(z + d, n_shard)),
+        )
+        c.start()
+        fourth.append(c)
+    for c in fourth:
+        c.wait()
+    for c in first + second + third:
+        c.wait_send()
+
+
+def momentum_kernel(perm_ref, factor_ref, momentum_ref, grad_ref, out_ref, u_ref):
+    q = pl.program_id(0)
+    factor = factor_ref[perm_ref[q]]
+    rows = grad_ref.shape[3]
+    for c in range(2):
+        cut = pl.ds(c * rows, rows)
+        step = factor * grad_ref[0, c, 0].astype(jnp.float32)
+        new = momentum_rate * momentum_ref[0, cut] + step
+        out_ref[0, cut] = new
+        u_ref[0, 0, cut] = (step + momentum_rate * new).astype(u_ref.dtype)
+
+
+def spread_kernel(n_shard, u_ref, full_ref, local_sem, zs, zr, cs, cr):
+    me, core, x, y, to_core, to_x, to_y, to_xy = place()
+    z = lax.axis_index("shard")
+    group = lax.div(me, 2)
+    rows = full_ref.shape[1] // 2
+    cols = full_ref.shape[2] // n_shard
+
+    def at(shard):
+        return full_ref.at[
+            :, pl.ds(pl.multiple_of(core * rows, rows), rows),
+            pl.ds(pl.multiple_of(shard * cols, cols), cols),
+        ]
+
+    local = pltpu.make_async_copy(
+        u_ref.at[group], full_ref.at[:, :, pl.ds(pl.multiple_of(z * cols, cols), cols)], local_sem
+    )
+    local.start()
+    greet([(to_core, z)] + [(me, lax.rem(z + d, n_shard)) for d in range(1, n_shard)])
+    mine = u_ref.at[group, :, pl.ds(pl.multiple_of(core * rows, rows), rows)]
+    order = [d for d in (2, 1, 3) if d < n_shard] + list(range(4, n_shard))
+    copies = []
+    for d in order:
+        c = remote(mine, at(z), zs.at[d - 1], zr.at[d - 1], (me, lax.rem(z + d, n_shard)))
+        c.start()
+        copies.append(c)
+    onward = []
+    for c, d in zip(copies, order):
+        c.wait_recv()
+        source = lax.rem(z + n_shard - d, n_shard)
+        f = remote(at(source), at(source), cs.at[d - 1], cr.at[d - 1], (to_core, z))
+        f.start()
+        onward.append(f)
+    for f in onward:
+        f.wait_recv()
+    for c in copies + onward:
+        c.wait_send()
+    local.wait()
+
+
+def newton_kernel(u_ref, o_ref):
+    def total(i, carry):
+        value = u_ref[0, pl.ds(pl.multiple_of(i * 32, 32), 32), :].astype(jnp.float32)
+        return carry + jnp.sum(value * value, axis=0, keepdims=True)
+
+    kv, width = u_ref.shape[1:]
+    sums = lax.fori_loop(0, kv // 32, total, jnp.zeros((1, width), jnp.float32))
+    inverse = 1.0 / (jnp.sqrt(jnp.sum(sums, axis=1, keepdims=True)) + epsilon)
+    matrix = (u_ref[0].astype(jnp.float32) * inverse).astype(jnp.bfloat16)
+    for iteration in range(ITERS):
+        gram = lax.dot_general(
+            matrix, matrix, (((1,), (1,)), ((), ())), preferred_element_type=jnp.float32
+        ).astype(jnp.bfloat16)
+        square = jnp.dot(gram, gram, preferred_element_type=jnp.float32)
+        mixing = (coef_b * gram.astype(jnp.float32) + coef_c * square).astype(jnp.bfloat16)
+        product = jnp.dot(mixing, matrix, preferred_element_type=jnp.float32)
+        matrix = (coef_a * matrix.astype(jnp.float32) + product).astype(jnp.bfloat16)
+    o_ref[0] = matrix
+
+
+def share_kernel(
+    n_shard, pick_ref, keep_ref, o_ref, oall_ref, whole_ref, us, ur, ws, wr
+):
+    me, core, x, y, to_core, to_x, to_y, to_xy = place()
+    z = lax.axis_index("shard")
+    group = lax.div(me, 2)
+    rows = o_ref.shape[1] // 2
+    cols = o_ref.shape[2] // n_shard
+    half = pl.ds(pl.multiple_of(core * rows, rows), rows)
+    for j in range(o_ref.shape[0]):
+        oall_ref[me, j] = o_ref[j, half, pl.ds(pl.multiple_of(z * cols, cols), cols)]
+    chosen = o_ref[pick_ref[0], half, :]
+    whole_ref[me] = (chosen.astype(jnp.float32) * keep_ref[0]).astype(whole_ref.dtype)
+    greet([(p, z) for p in (to_core, to_x, to_y, to_xy)])
+    at_u = lambda r: oall_ref.at[r]
+    at_w = lambda r: whole_ref.at[r]
+    cu = plane_gather_start(z, at_u, us, ur)
+    cw = plane_gather_start(z, at_w, ws, wr)
+    plane_gather_finish(z, at_u, us, ur, cu)
+    plane_gather_finish(z, at_w, ws, wr, cw)
+
+
+def update_kernel(scale, perm_ref, o_ref, out_ref):
+    rows = o_ref.shape[3]
+    for c in range(2):
+        out_ref[0, pl.ds(c * rows, rows)] = scale * o_ref[0, c, 0].astype(jnp.float32)
+
+
+def owned_kernel(scale, index_ref, keep_ref, w_ref, out_ref):
+    rows = w_ref.shape[2]
+    keep = keep_ref[pl.program_id(0)]
+    for c in range(2):
+        value = scale * w_ref[0, c].astype(jnp.float32)
+        out_ref[0, pl.ds(c * rows, rows)] = (value * keep).astype(out_ref.dtype)
+
+
+def per_device_planes(activations, cotangents, momentum, owners, bucket_starts):
+    n_shard = lax.axis_size("shard")
+    n_rep = lax.axis_size("rep")
+    layers, tok_rows, width = activations.shape
+    token_total = tok_rows * n_shard * n_rep
+    cols = width // n_shard
+    rows = KV // 2
+    groups = n_rep // 2
+    members = MATS // groups
+    slots = -(-MATS // n_shard) + 1
+    update_scale = math.sqrt(max(KV, D))
+    bf16, f32, i32 = jnp.bfloat16, jnp.float32, jnp.int32
+    z = lax.axis_index("shard")
+    my_group = lax.axis_index("rep") // 2
+
+    index = jnp.arange(MATS, dtype=i32)
+    before = (owners[None, :] < owners[:, None]) | (
+        (owners[None, :] == owners[:, None]) & (index[None, :] < index[:, None])
+    )
+    rank = jnp.sum(before.astype(i32), axis=1)
+    position = (rank % groups) * members + rank // groups
+    perm = jnp.sum(jnp.where(position[None, :] == index[:, None], index[None, :], 0), axis=1)
+    start = jnp.sum((owners < z).astype(i32))
+    count = jnp.sum((owners == z).astype(i32))
+
+    params = functools.partial(
+        pltpu.CompilerParams, has_side_effects=True, vmem_limit_bytes=VMEM_LIMIT
+    )
+    dma = pltpu.SemaphoreType.DMA
+    gall, sq = pl.pallas_call(
+        functools.partial(reduce_kernel, n_shard, 1.0 / math.sqrt(token_total)),
+        out_shape=(
+            jax.ShapeDtypeStruct((n_rep, members, rows, cols), bf16),
+            jax.ShapeDtypeStruct((n_shard, n_rep, members, 1, cols), f32),
+        ),
+        in_specs=[SMEM_SPEC, SMEM_SPEC, ANY_SPEC, ANY_SPEC],
+        out_specs=(VMEM_SPEC, VMEM_SPEC),
+        scratch_shapes=[
+            pltpu.VMEM((layers, 2 * tok_rows, width), bf16),
+            pltpu.VMEM((layers, 2 * tok_rows, 2 * KV), bf16),
+            pltpu.VMEM((n_shard, 2, 2, members, rows, cols), bf16),
+            pltpu.VMEM((n_shard, 2, members, rows, cols), bf16),
+            pltpu.VMEM((n_shard, members, rows, cols), bf16),
+            pltpu.VMEM((n_shard, members, rows, cols), bf16),
+            pltpu.VMEM((n_shard, members, rows, cols), bf16),
+            pltpu.VMEM((n_shard - 1, members, rows, cols), bf16),
+            dma((2,)), dma((2,)), dma((2,)),
+            dma((n_shard,)), dma((n_shard,)), dma((n_shard,)), dma((n_shard,)),
+            dma((n_shard,)), dma((n_shard,)),
+            dma((7,)), dma((7,)), dma((n_shard - 1,)), dma((n_shard - 1,)),
+        ],
+        compiler_params=params(collective_id=0),
+        name="reduce",
+    )(perm // 2, perm % 2, activations, cotangents)
+
+    by_position = jnp.sum(
+        sq.reshape(n_shard, groups, 2, members, cols), axis=(0, 2, 4)
+    ).reshape(MATS)
+    square_sums = jnp.sum(
+        jnp.where(position[:, None] == index[None, :], by_position[None, :], 0.0), axis=1
+    )
+    factors = clip_factors(square_sums, bucket_starts)
+
+    momentum_out, nesterov = pl.pallas_call(
+        momentum_kernel,
+        out_shape=(
+            jax.ShapeDtypeStruct(momentum.shape, f32),
+            jax.ShapeDtypeStruct((groups, members, KV, cols), bf16),
+        ),
+        grid_spec=pltpu.PrefetchScalarGridSpec(
+            num_scalar_prefetch=2,
+            grid=(MATS,),
+            in_specs=[
+                pl.BlockSpec((1, KV, cols), lambda q, p, f: (p[q], 0, 0)),
+                pl.BlockSpec(
+                    (1, 2, 1, rows, cols), lambda q, p, f: (q // members, 0, q % members, 0, 0)
+                ),
+            ],
+            out_specs=(
+                pl.BlockSpec((1, KV, cols), lambda q, p, f: (p[q], 0, 0)),
+                pl.BlockSpec((1, 1, KV, cols), lambda q, p, f: (q // members, q % members, 0, 0)),
+            ),
+        ),
+        name="momentum",
+    )(perm, factors, momentum, gall.reshape(groups, 2, members, rows, cols))
+
+    full = pl.pallas_call(
+        functools.partial(spread_kernel, n_shard),
+        out_shape=jax.ShapeDtypeStruct((members, KV, width), bf16),
+        in_specs=[ANY_SPEC],
+        out_specs=VMEM_SPEC,
+        scratch_shapes=[dma(())] + [dma((n_shard - 1,)) for _ in range(4)],
+        compiler_params=params(collective_id=1),
+        name="spread",
+    )(nesterov)
+
+    result = pl.pallas_call(
+        newton_kernel,
+        out_shape=jax.ShapeDtypeStruct((members, KV, width), bf16),
+        grid=(members,),
+        in_specs=[pl.BlockSpec((1, KV, width), lambda i: (i, 0, 0))],
+        out_specs=pl.BlockSpec((1, KV, width), lambda i: (i, 0, 0)),
+        name="newton",
+    )(full)
+
+    mine = start + (my_group - start) % groups
+    keep = (mine < start + count).astype(f32)
+    pick = jnp.minimum(mine // groups, members - 1)
+    oall, whole = pl.pallas_call(
+        functools.partial(share_kernel, n_shard),
+        out_shape=(
+            jax.ShapeDtypeStruct((n_rep, members, rows, cols), bf16),
+            jax.ShapeDtypeStruct((n_rep, rows, width), bf16),
+        ),
+        in_specs=[SMEM_SPEC, SMEM_SPEC, VMEM_SPEC],
+        out_specs=(VMEM_SPEC, VMEM_SPEC),
+        scratch_shapes=[dma((7,)) for _ in range(4)],
+        compiler_params=params(collective_id=2),
+        name="share",
+    )(pick.reshape(1), keep.reshape(1), result)
+
+    update = pl.pallas_call(
+        functools.partial(update_kernel, update_scale),
+        out_shape=jax.ShapeDtypeStruct(momentum.shape, f32),
+        grid_spec=pltpu.PrefetchScalarGridSpec(
+            num_scalar_prefetch=1,
+            grid=(MATS,),
+            in_specs=[
+                pl.BlockSpec(
+                    (1, 2, 1, rows, cols), lambda q, p: (q // members, 0, q % members, 0, 0)
+                )
+            ],
+            out_specs=pl.BlockSpec((1, KV, cols), lambda q, p: (p[q], 0, 0)),
+        ),
+        name="update",
+    )(perm, oall.reshape(groups, 2, members, rows, cols))
+
+    slot = jnp.arange(slots, dtype=i32)
+    owned = pl.pallas_call(
+        functools.partial(owned_kernel, update_scale),
+        out_shape=jax.ShapeDtypeStruct((slots, KV, width), bf16),
+        grid_spec=pltpu.PrefetchScalarGridSpec(
+            num_scalar_prefetch=2,
+            grid=(slots,),
+            in_specs=[pl.BlockSpec((1, 2, rows, width), lambda s, i, k: (i[s], 0, 0, 0))],
+            out_specs=pl.BlockSpec((1, KV, width), lambda s, i, k: (s, 0, 0)),
+        ),
+        name="owned",
+    )(
+        (start + slot) % groups,
+        (slot < count).astype(f32),
+        whole.reshape(groups, 2, rows, width),
+    )
+    return (momentum_out, update, owned)
+
+
 def solution(mesh):
+    groups = mesh.shape["rep"] // 2
+    slots = -(-MATS // mesh.shape["shard"]) + 1
+    fits = mesh.shape["rep"] == 8 and MATS % groups == 0 and slots <= groups
     placed = (
         P(None, ("rep", "shard"), None),
         P(None, ("rep", "shard"), None),
@@ -119,7 +569,7 @@
         P(),
     )
     return jax.shard_map(
-        per_device,
+        per_device_planes if fits else per_device_general,
         mesh=mesh,
         in_specs=placed,
         out_specs=(P(None, None, "shard"), P(None, None, "shard"), P("shard", None, None)),

time: 630 us -> 277 us (0.44)
  waiting for transfers between devices: 286 us -> 0 us
  Pallas kernels: 0 us -> 265 us
  blocking collectives: 197 us -> 0 us
  matrix products: 66.7 us -> 0 us
  local copies, waits for them, and re-layouts: 39.3 us -> 0.09 us
  other arithmetic: 19.4 us -> 8.13 us
  between operations: 14.1 us -> 3.31 us
    pallas_call x0 -> x7, Pallas kernels: none -> 265 us  [the longest x1 122 us: per_device_planes(): pl.pallas_call(functools.partial(reduce_kernel, n_shard, 1.0 / math.sqrt(...]
    reduce_scatter x1 -> x0, waiting for transfers between devices: 214 us -> none  [per_device(): lax.psum_scatter(partial_terms.astype(jnp.bfloat16), 'shard', scatter_dim...]
    all_to_all x2 -> x0, blocking collectives: 191 us -> none  [the longest x1 95.9 us: per_device(): lax.all_to_all(pack_slots(nesterov, chooser), 'shard', split_axis=2, conc...]
    psum x1 -> x0, waiting for transfers between devices: 72.2 us -> none  [per_device(): summed = lax.psum(shard_part, 'rep').astype(jnp.float32)]
    dot_general x13 -> x0, matrix products: 66.7 us -> none  [the longest x5 32.7 us: orthogonal_batch(): jnp.einsum('skj,sjd->skd', mixing, matrix, preferred_element_type=jnp.flo...]
    reshape x2 -> x0, local copies, waits for them, and re-layouts: 13.2 us -> none  [per_device(): result.reshape(item_count, KV, shard_count, columns)]
    convert_element_type x2 -> x1, other arithmetic: 12.7 us -> 1.23 us  [per_device_planes(): (slot < count).astype(f32)]
    unnamed x11 -> x2, local copies, waits for them, and re-layouts: 10.2 us -> 0.01 us
  transfers between devices with their start and end apart: 2 -> 0, of which waited for: 2 -> 0; matrix products, arithmetic and copies ran while one was open for 0% -> 0% of each run, Pallas kernels for 0% -> 0%
where the time goes in v1:
time: 277 us
  Pallas kernels  265 us (96%)
  other arithmetic  8.13 us (3%)
  between operations  3.31 us (1%)
    pallas_call x1, Pallas kernels, per_device_planes(): pl.pallas_call(functools.partial(reduce_kernel, n_shard, 1.0 / math.sqrt(...  122 us
    pallas_call x1, Pallas kernels, per_device_planes(): pl.pallas_call(functools.partial(share_kernel, n_shard), out_shape=(jax.S...  50.9 us
    pallas_call x1, Pallas kernels, per_device_planes(): pl.pallas_call(functools.partial(spread_kernel, n_shard), out_shape=jax.S...  43.2 us
    pallas_call x1, Pallas kernels, per_device_planes(): pl.pallas_call(newton_kernel, out_shape=jax.ShapeDtypeStruct((members, KV...  22.1 us
    pallas_call x1, Pallas kernels, per_device_planes(): pl.pallas_call(momentum_kernel, out_shape=(jax.ShapeDtypeStruct(momentum....  12.3 us
    pallas_call x1, Pallas kernels, per_device_planes(): pl.pallas_call(functools.partial(update_kernel, update_scale), out_shape=...  9.14 us
    pallas_call x1, Pallas kernels, per_device_planes(): pl.pallas_call(functools.partial(owned_kernel, update_scale), out_shape=j...  5.72 us

profile of v1, /device:TPU:17, one launch (start us, length us, event | category | flops | bytes accessed | tf_op | source)
XLA Modules:
  0.0 276.6 jit_solution(9802226074795890155)
XLA Ops:
  0.6 0.7 fusion.4
  1.4 0.9 convert_reduce_fusion
  2.3 0.1 select_reduce_fusion.1.perm_ref
  2.4 0.0 copy-start
  2.4 1.3 fusion.8
  6.4 1.2 compare_convert_fusion.1.keep_ref
  7.6 1.2 and_select_fusion.index_ref
  8.8 0.5 and_select_fusion.1
  9.3 121.6 %reduce.3 = (bf16[8,3,128,512]{3,2,1,0:T(8,128)(2,1)}, f32[4,8,3,1,512]{4,3,2,1,0:T(1,128)}) custom-call(s32[12]{0:T(128)} %get-tuple-element.20.lay_ref, s32[12]{0:T(128)} %get-tuple-element.19.half_ref, bf16[6,128,2048]{2,1,0:T(8,128)(2,1)} %act_ref.1, bf16[6,128,512]{2,1,0:T(8,128)(2,1)} %cot_ref.1), custom_call_target="tpu_custom_call" | custom-call | tf_op jit(solution)/shard_map/reduce/pallas_call | solution.py:433
  131.0 1.1 reduce_sum.91
  132.1 0.1 broadcast_in_dim.21
  132.2 0.2 select_reduce_fusion
  132.4 0.2 fusion.1
  132.6 0.5 multiply_minimum_fusion.factor_ref
  133.1 0.0 copy-done
  133.1 12.3 %momentum.1 = (f32[12,256,512]{2,1,0:T(8,128)}, bf16[4,3,256,512]{3,2,1,0:T(8,128)(2,1)}) custom-call(s32[12]{0:T(128)} %copy-done, f32[12]{0:T(128)} %multiply_minimum_fusion.factor_ref, f32[12,256,512]{2,1,0:T(8,128)} %momentum_ref.1, bf16[4,2,3,128,512]{4,3,2,1,0:T(8,128)(2,1)} %bitcast.7), custom_call_target="tpu_custom_call" | custom-call | tf_op jit(solution)/shard_map/momentum/pallas_call | solution.py:467
  145.4 43.2 %spread.1.u_ref = bf16[3,256,2048]{2,1,0:T(8,128)(2,1)} custom-call(bf16[4,3,256,512]{3,2,1,0:T(8,128)(2,1)} %get-tuple-element.12.u_ref), custom_call_target="tpu_custom_call" | custom-call | tf_op jit(solution)/shard_map/spread/pallas_call | solution.py:490
  188.7 22.1 %newton.1.o_ref = bf16[3,256,2048]{2,1,0:T(8,128)(2,1)} custom-call(bf16[3,256,2048]{2,1,0:T(8,128)(2,1)} %spread.1.u_ref), custom_call_target="tpu_custom_call" | custom-call | tf_op jit(solution)/shard_map/newton/pallas_call | solution.py:500
  210.8 50.9 %share.1 = (bf16[8,3,128,512]{3,2,1,0:T(8,128)(2,1)}, bf16[8,128,2048]{2,1,0:T(8,128)(2,1)}) custom-call(s32[1]{0:T(128)} %bitcast.2.pick_ref, f32[1]{0:T(128)} %bitcast.3.keep_ref, bf16[3,256,2048]{2,1,0:T(8,128)(2,1)} %newton.1.o_ref), custom_call_target="tpu_custom_call" | custom-call | tf_op jit(solution)/shard_map/share/pallas_call | solution.py:512
  261.7 5.7 %owned.1 = bf16[4,256,2048]{2,1,0:T(8,128)(2,1)} custom-call(s32[4]{0:T(128)} %and_select_fusion.index_ref, f32[4]{0:T(128)} %compare_convert_fusion.1.keep_ref, bf16[4,2,128,2048]{3,2,1,0:T(8,128)(2,1)} %bitcast.6), custom_call_target="tpu_custom_call" | custom-call | tf_op jit(solution)/shard_map/owned/pallas_call | solution.py:542
  267.4 9.1 %update.1 = f32[12,256,512]{2,1,0:T(8,128)} custom-call(s32[12]{0:T(128)} %copy-done, bf16[4,2,3,128,512]{4,3,2,1,0:T(8,128)(2,1)} %bitcast.8), custom_call_target="tpu_custom_call" | custom-call | tf_op jit(solution)/shard_map/update/pallas_call | solution.py:525
  (2 shorter events, 0.0 us)
Async XLA Ops:
  2.4 130.7 %copy-start = (s32[12]{0:T(128)}, s32[12]{0:T(128)S(1)}, u32[]{:S(2)}) copy-start(s32[12]{0:T(128)S(1)} %select_reduce_fusion.1.perm_ref) | copy-start | bytes 148

commit v2 on v1

--- a/solution.py
+++ b/solution.py
@@ -142,27 +142,59 @@
     )
 
 
-def plane_gather_start(z, buf_at, send, recv):
+def plane_gather_start(z, at, send, recv):
     me, core, x, y, to_core, to_x, to_y, to_xy = place()
-    copies = []
-    for k, peer in enumerate((to_x, to_y, to_xy, to_core)):
-        c = remote(buf_at(me), buf_at(me), send.at[k], recv.at[k], (peer, z))
-        c.start()
-        copies.append(c)
+    plan = ((0, to_x, 0), (2, to_y, 1), (1, to_x, 1), (3, to_y, 0), (4, to_core, None))
+    copies = {}
+    for k, peer, half in plan:
+        copies[k] = remote(at(me, half), at(me, half), send.at[k], recv.at[k], (peer, z))
+        copies[k].start()
     return copies
 
 
-def plane_gather_finish(z, buf_at, send, recv, copies):
+def plane_gather_turn(z, at, send, recv, copies):
     me, core, x, y, to_core, to_x, to_y, to_xy = place()
-    for k, source in enumerate((to_x, to_y, to_xy)):
+
+    def forward(k, block, half, peer):
+        copies[k] = remote(
+            at(block, half), at(block, half), send.at[k], recv.at[k], (peer, z)
+        )
+        copies[k].start()
+
+    copies[0].wait_recv()
+    forward(5, to_x, 0, to_y)
+    copies[2].wait_recv()
+    forward(6, to_y, 1, to_x)
+    copies[1].wait_recv()
+    forward(7, to_x, None, to_core)
+    copies[3].wait_recv()
+    forward(8, to_y, None, to_core)
+
+
+def plane_gather_finish(z, at, send, recv, copies):
+    me, core, x, y, to_core, to_x, to_y, to_xy = place()
+    copies[5].wait_recv()
+    copies[6].wait_recv()
+    copies[9] = remote(
+        at(to_xy, None), at(to_xy, None), send.at[9], recv.at[9], (to_core, z)
+    )
+    copies[9].start()
+    for k in (4, 7, 8, 9):
         copies[k].wait_recv()
-        c = remote(buf_at(source), buf_at(source), send.at[4 + k], recv.at[4 + k], (to_core, z))
-        c.start()
-        copies.append(c)
-    for k in range(3, 7):
-        copies[k].wait_recv()
-    for c in copies:
-        c.wait_send()
+    for k in range(10):
+        copies[k].wait_send()
+
+
+def block_at(ref, axis):
+    rows = ref.shape[axis] // 2
+
+    def at(r, half):
+        if half is None:
+            return ref.at[r]
+        cut = pl.ds(half * rows, rows)
+        return ref.at[r, cut] if axis == 1 else ref.at[r, :, cut]
+
+    return at
 
 
 def reduce_kernel(
@@ -196,10 +228,13 @@
     for c in swap:
         c.wait()
     first = []
-    for k, d in enumerate(steps):
-        offset = pl.multiple_of(lax.rem(z + d, n_shard) * cols, cols)
-
-        def one(q, carry, k=k, offset=offset):
+    second = []
+    third = []
+
+    def launch(k):
+        offset = pl.multiple_of(lax.rem(z + steps[k], n_shard) * cols, cols)
+
+        def one(q, carry):
             group = lax.div(q, members)
             member = lax.rem(q, members)
             block = cot[lay_ref[q]]
@@ -214,17 +249,19 @@
             return carry
 
         lax.fori_loop(0, 4 * members, one, 0)
+
+    def send_first(k):
         if k % 2 == 0:
             c = remote(part.at[k, :, 1 - x], recv1.at[k], s1.at[k], r1.at[k], (to_x, z))
         else:
             c = remote(part.at[k, 1 - y], recv1.at[k], s1.at[k], r1.at[k], (to_y, z))
         c.start()
         first.append(c)
-    second = []
-    for k in range(n_shard):
+
+    def send_second(k):
         first[k].wait_recv()
 
-        def add_out(j, carry, k=k):
+        def add_out(j, carry):
             if k % 2 == 0:
                 mine = part[k, 1 - y, x, j]
                 came = recv1[k, 1 - y, j]
@@ -240,11 +277,11 @@
         )
         c.start()
         second.append(c)
-    third = []
-    for k, d in enumerate(steps):
+
+    def send_third(k):
         second[k].wait_recv()
 
-        def add_in(j, carry, k=k):
+        def add_in(j, carry):
             came = recv1[k, y, j] if k % 2 == 0 else recv1[k, x, j]
             value = part[k, y, x, j].astype(jnp.float32) + came.astype(jnp.float32)
             value = value + recv2[k, j].astype(jnp.float32)
@@ -252,12 +289,29 @@
             return carry
 
         lax.fori_loop(0, members, add_in, 0)
-        if d:
+        if steps[k]:
             c = remote(
-                plane.at[k], zrecv.at[k], s3.at[k], r3.at[k], (me, lax.rem(z + d, n_shard))
+                plane.at[k], zrecv.at[k], s3.at[k], r3.at[k],
+                (me, lax.rem(z + steps[k], n_shard)),
             )
             c.start()
             third.append(c)
+
+    launch(0)
+    send_first(0)
+    launch(1)
+    send_first(1)
+    for k in range(2, n_shard):
+        launch(k)
+    for k in range(0, n_shard, 2):
+        pair = [i for i in (k, k + 1) if i < n_shard]
+        for i in pair:
+            send_second(i)
+        for i in (k + 2, k + 3):
+            if i < n_shard:
+                send_first(i)
+        for i in pair:
+            send_third(i)
     for c in third:
         c.wait_recv()
 
@@ -269,8 +323,9 @@
         return carry
 
     lax.fori_loop(0, members, add_last, 0)
-    at = lambda r: gall_ref.at[r]
+    at = block_at(gall_ref, 2)
     copies = plane_gather_start(z, at, gs, gr)
+    plane_gather_turn(z, at, gs, gr, copies)
     plane_gather_finish(z, at, gs, gr, copies)
 
     def square(r, carry):
@@ -294,66 +349,63 @@
         c.wait_send()
 
 
-def momentum_kernel(perm_ref, factor_ref, momentum_ref, grad_ref, out_ref, u_ref):
-    q = pl.program_id(0)
-    factor = factor_ref[perm_ref[q]]
-    rows = grad_ref.shape[3]
-    for c in range(2):
-        cut = pl.ds(c * rows, rows)
-        step = factor * grad_ref[0, c, 0].astype(jnp.float32)
-        new = momentum_rate * momentum_ref[0, cut] + step
-        out_ref[0, cut] = new
-        u_ref[0, 0, cut] = (step + momentum_rate * new).astype(u_ref.dtype)
-
-
-def spread_kernel(n_shard, u_ref, full_ref, local_sem, zs, zr, cs, cr):
+def spread_kernel(
+    n_shard, mat_ref, place_ref, factor_ref, momentum_ref, gall_ref, full_ref,
+    held, zs, zr, cs, cr,
+):
     me, core, x, y, to_core, to_x, to_y, to_xy = place()
     z = lax.axis_index("shard")
-    group = lax.div(me, 2)
-    rows = full_ref.shape[1] // 2
-    cols = full_ref.shape[2] // n_shard
-
-    def at(shard):
-        return full_ref.at[
-            :, pl.ds(pl.multiple_of(core * rows, rows), rows),
+    block = me - core
+    rows = full_ref.shape[0] // 2
+    cols = full_ref.shape[1] // n_shard
+
+    def at(side, shard):
+        return (
+            pl.ds(pl.multiple_of(side * rows, rows), rows),
             pl.ds(pl.multiple_of(shard * cols, cols), cols),
-        ]
-
-    local = pltpu.make_async_copy(
-        u_ref.at[group], full_ref.at[:, :, pl.ds(pl.multiple_of(z * cols, cols), cols)], local_sem
-    )
-    local.start()
+        )
+
+    def nesterov(p, side):
+        matrix = mat_ref[p]
+        half = pl.ds(pl.multiple_of(side * rows, rows), rows)
+        step = factor_ref[matrix] * gall_ref[block + side, place_ref[p]].astype(jnp.float32)
+        new = momentum_rate * momentum_ref[matrix, half] + step
+        return (step + momentum_rate * new).astype(full_ref.dtype)
+
+    order = [d for d in (2, 1, 3) if d < n_shard] + list(range(4, n_shard))
+    for d in order:
+        held[d - 1] = nesterov(lax.rem(z + d, n_shard), core)
     greet([(to_core, z)] + [(me, lax.rem(z + d, n_shard)) for d in range(1, n_shard)])
-    mine = u_ref.at[group, :, pl.ds(pl.multiple_of(core * rows, rows), rows)]
-    order = [d for d in (2, 1, 3) if d < n_shard] + list(range(4, n_shard))
     copies = []
     for d in order:
-        c = remote(mine, at(z), zs.at[d - 1], zr.at[d - 1], (me, lax.rem(z + d, n_shard)))
+        peer = (me, lax.rem(z + d, n_shard))
+        c = remote(held.at[d - 1], full_ref.at[at(core, z)], zs.at[d - 1], zr.at[d - 1], peer)
         c.start()
         copies.append(c)
+    for side in range(2):
+        full_ref[at(side, z)] = nesterov(z, side)
     onward = []
     for c, d in zip(copies, order):
         c.wait_recv()
-        source = lax.rem(z + n_shard - d, n_shard)
-        f = remote(at(source), at(source), cs.at[d - 1], cr.at[d - 1], (to_core, z))
+        source = full_ref.at[at(core, lax.rem(z + n_shard - d, n_shard))]
+        f = remote(source, source, cs.at[d - 1], cr.at[d - 1], (to_core, z))
         f.start()
         onward.append(f)
     for f in onward:
         f.wait_recv()
     for c in copies + onward:
         c.wait_send()
-    local.wait()
 
 
 def newton_kernel(u_ref, o_ref):
     def total(i, carry):
-        value = u_ref[0, pl.ds(pl.multiple_of(i * 32, 32), 32), :].astype(jnp.float32)
+        value = u_ref[pl.ds(pl.multiple_of(i * 32, 32), 32), :].astype(jnp.float32)
         return carry + jnp.sum(value * value, axis=0, keepdims=True)
 
-    kv, width = u_ref.shape[1:]
+    kv, width = u_ref.shape
     sums = lax.fori_loop(0, kv // 32, total, jnp.zeros((1, width), jnp.float32))
     inverse = 1.0 / (jnp.sqrt(jnp.sum(sums, axis=1, keepdims=True)) + epsilon)
-    matrix = (u_ref[0].astype(jnp.float32) * inverse).astype(jnp.bfloat16)
+    matrix = (u_ref[...].astype(jnp.float32) * inverse).astype(jnp.bfloat16)
     for iteration in range(ITERS):
         gram = lax.dot_general(
             matrix, matrix, (((1,), (1,)), ((), ())), preferred_element_type=jnp.float32
@@ -362,43 +414,99 @@
         mixing = (coef_b * gram.astype(jnp.float32) + coef_c * square).astype(jnp.bfloat16)
         product = jnp.dot(mixing, matrix, preferred_element_type=jnp.float32)
         matrix = (coef_a * matrix.astype(jnp.float32) + product).astype(jnp.bfloat16)
-    o_ref[0] = matrix
+    o_ref[...] = matrix
 
 
 def share_kernel(
-    n_shard, pick_ref, keep_ref, o_ref, oall_ref, whole_ref, us, ur, ws, wr
+    n_shard, owner_ref, o_ref, oall_ref, whole_ref, back, bs, br, us, ur, ws, wr
 ):
     me, core, x, y, to_core, to_x, to_y, to_xy = place()
     z = lax.axis_index("shard")
-    group = lax.div(me, 2)
-    rows = o_ref.shape[1] // 2
-    cols = o_ref.shape[2] // n_shard
+    rows = o_ref.shape[0] // 2
+    cols = o_ref.shape[1] // n_shard
     half = pl.ds(pl.multiple_of(core * rows, rows), rows)
-    for j in range(o_ref.shape[0]):
-        oall_ref[me, j] = o_ref[j, half, pl.ds(pl.multiple_of(z * cols, cols), cols)]
-    chosen = o_ref[pick_ref[0], half, :]
-    whole_ref[me] = (chosen.astype(jnp.float32) * keep_ref[0]).astype(whole_ref.dtype)
-    greet([(p, z) for p in (to_core, to_x, to_y, to_xy)])
-    at_u = lambda r: oall_ref.at[r]
-    at_w = lambda r: whole_ref.at[r]
+
+    def piece(shard):
+        return half, pl.ds(pl.multiple_of(shard * cols, cols), cols)
+
+    peers = [(p, z) for p in (to_core, to_x, to_y)]
+    peers += [(me, lax.rem(z + d, n_shard)) for d in range(1, n_shard)]
+    greet(peers)
+    order = [d for d in (2, 1, 3) if d < n_shard] + list(range(4, n_shard))
+    returns = []
+    for d in order:
+        to = lax.rem(z + d, n_shard)
+        c = remote(o_ref.at[piece(to)], back.at[z], bs.at[d - 1], br.at[d - 1], (me, to))
+        c.start()
+        returns.append(c)
+    whole_ref[me] = o_ref[half]
+    at_w = block_at(whole_ref, 1)
+    at_u = block_at(oall_ref, 2)
+    cw = plane_gather_start(z, at_w, ws, wr)
+    back[z] = o_ref[piece(z)]
+    for c in returns:
+        c.wait_recv()
+    for j in range(oall_ref.shape[1]):
+        oall_ref[me, j] = back[owner_ref[j]]
     cu = plane_gather_start(z, at_u, us, ur)
-    cw = plane_gather_start(z, at_w, ws, wr)
+    plane_gather_turn(z, at_w, ws, wr, cw)
+    plane_gather_turn(z, at_u, us, ur, cu)
+    plane_gather_finish(z, at_w, ws, wr, cw)
     plane_gather_finish(z, at_u, us, ur, cu)
-    plane_gather_finish(z, at_w, ws, wr, cw)
-
-
-def update_kernel(scale, perm_ref, o_ref, out_ref):
-    rows = o_ref.shape[3]
-    for c in range(2):
-        out_ref[0, pl.ds(c * rows, rows)] = scale * o_ref[0, c, 0].astype(jnp.float32)
-
-
-def owned_kernel(scale, index_ref, keep_ref, w_ref, out_ref):
-    rows = w_ref.shape[2]
-    keep = keep_ref[pl.program_id(0)]
-    for c in range(2):
-        value = scale * w_ref[0, c].astype(jnp.float32)
-        out_ref[0, pl.ds(c * rows, rows)] = (value * keep).astype(out_ref.dtype)
+    for c in returns:
+        c.wait_send()
+
+
+def finish_kernel(
+    scale, block_ref, member_ref, factor_ref, slot_ref, keep_ref,
+    gall_ref, oall_ref, whole_ref, momentum_ref, mout_ref, update_ref, owned_ref,
+    mbuf, ubuf, wbuf, load, msem, usem, wsem,
+):
+    mats = mbuf.shape[0]
+    slots = wbuf.shape[0]
+    rows = gall_ref.shape[2]
+
+    def fetch(m):
+        return pltpu.make_async_copy(momentum_ref.at[m], mbuf.at[m], load.at[m])
+
+    def put(buf, out, sem, m):
+        return pltpu.make_async_copy(buf.at[m], out.at[m], sem.at[m])
+
+    def each(count, body):
+        def step(m, carry):
+            body(m)
+            return carry
+
+        lax.fori_loop(0, count, step, 0)
+
+    each(mats, lambda m: fetch(m).start())
+
+    def owned_one(s):
+        for c in range(2):
+            value = scale * whole_ref[slot_ref[s] + c].astype(jnp.float32)
+            wbuf[s, pl.ds(c * rows, rows)] = (value * keep_ref[s]).astype(wbuf.dtype)
+        put(wbuf, owned_ref, wsem, s).start()
+
+    def update_one(m):
+        for c in range(2):
+            value = oall_ref[block_ref[m] + c, member_ref[m]].astype(jnp.float32)
+            ubuf[m, pl.ds(c * rows, rows)] = scale * value
+        put(ubuf, update_ref, usem, m).start()
+
+    def momentum_one(m):
+        fetch(m).wait()
+        for c in range(2):
+            cut = pl.ds(c * rows, rows)
+            step = factor_ref[m] * gall_ref[block_ref[m] + c, member_ref[m]].astype(jnp.float32)
+            mbuf[m, cut] = momentum_rate * mbuf[m, cut] + step
+        put(mbuf, mout_ref, msem, m).start()
+
+    each(slots, owned_one)
+    each(mats, update_one)
+    each(mats, momentum_one)
+    each(slots, lambda s: put(wbuf, owned_ref, wsem, s).wait())
+    each(mats, lambda m: put(ubuf, update_ref, usem, m).wait())
+    each(mats, lambda m: put(mbuf, mout_ref, msem, m).wait())
 
 
 def per_device_planes(activations, cotangents, momentum, owners, bucket_starts):
@@ -450,7 +558,7 @@
             dma((2,)), dma((2,)), dma((2,)),
             dma((n_shard,)), dma((n_shard,)), dma((n_shard,)), dma((n_shard,)),
             dma((n_shard,)), dma((n_shard,)),
-            dma((7,)), dma((7,)), dma((n_shard - 1,)), dma((n_shard - 1,)),
+            dma((10,)), dma((10,)), dma((n_shard - 1,)), dma((n_shard - 1,)),
         ],
         compiler_params=params(collective_id=0),
         name="reduce",
@@ -464,95 +572,74 @@
     )
     factors = clip_factors(square_sums, bucket_starts)
 
-    momentum_out, nesterov = pl.pallas_call(
-        momentum_kernel,
-        out_shape=(
-            jax.ShapeDtypeStruct(momentum.shape, f32),
-            jax.ShapeDtypeStruct((groups, members, KV, cols), bf16),
-        ),
-        grid_spec=pltpu.PrefetchScalarGridSpec(
-            num_scalar_prefetch=2,
-            grid=(MATS,),
-            in_specs=[
-                pl.BlockSpec((1, KV, cols), lambda q, p, f: (p[q], 0, 0)),
-                pl.BlockSpec(
-                    (1, 2, 1, rows, cols), lambda q, p, f: (q // members, 0, q % members, 0, 0)
-                ),
-            ],
-            out_specs=(
-                pl.BlockSpec((1, KV, cols), lambda q, p, f: (p[q], 0, 0)),
-                pl.BlockSpec((1, 1, KV, cols), lambda q, p, f: (q // members, q % members, 0, 0)),
-            ),
-        ),
-        name="momentum",
-    )(perm, factors, momentum, gall.reshape(groups, 2, members, rows, cols))
-
+    planes = jnp.arange(n_shard, dtype=i32)
+    firsts = jnp.sum((owners[None, :] < planes[:, None]).astype(i32), axis=1)
+    ranks = jnp.minimum(firsts + (my_group - firsts) % groups, MATS - 1)
+    places = ranks // groups
+    at_place = my_group * members + places
+    mats = jnp.sum(
+        jnp.where(position[None, :] == at_place[:, None], index[None, :], 0), axis=1
+    )
     full = pl.pallas_call(
         functools.partial(spread_kernel, n_shard),
-        out_shape=jax.ShapeDtypeStruct((members, KV, width), bf16),
-        in_specs=[ANY_SPEC],
+        out_shape=jax.ShapeDtypeStruct((KV, width), bf16),
+        in_specs=[SMEM_SPEC, SMEM_SPEC, SMEM_SPEC, VMEM_SPEC, VMEM_SPEC],
         out_specs=VMEM_SPEC,
-        scratch_shapes=[dma(())] + [dma((n_shard - 1,)) for _ in range(4)],
+        scratch_shapes=[pltpu.VMEM((n_shard - 1, rows, cols), bf16)]
+        + [dma((n_shard - 1,)) for _ in range(4)],
         compiler_params=params(collective_id=1),
         name="spread",
-    )(nesterov)
+    )(mats, places, factors, momentum, gall)
 
     result = pl.pallas_call(
         newton_kernel,
-        out_shape=jax.ShapeDtypeStruct((members, KV, width), bf16),
-        grid=(members,),
-        in_specs=[pl.BlockSpec((1, KV, width), lambda i: (i, 0, 0))],
-        out_specs=pl.BlockSpec((1, KV, width), lambda i: (i, 0, 0)),
+        out_shape=jax.ShapeDtypeStruct((KV, width), bf16),
+        in_specs=[VMEM_SPEC],
+        out_specs=VMEM_SPEC,
         name="newton",
     )(full)
 
-    mine = start + (my_group - start) % groups
-    keep = (mine < start + count).astype(f32)
-    pick = jnp.minimum(mine // groups, members - 1)
+    member = my_group * members + jnp.arange(members, dtype=i32)
+    owner = jnp.sum(
+        jnp.where(position[None, :] == member[:, None], owners[None, :], 0), axis=1
+    )
     oall, whole = pl.pallas_call(
         functools.partial(share_kernel, n_shard),
         out_shape=(
             jax.ShapeDtypeStruct((n_rep, members, rows, cols), bf16),
             jax.ShapeDtypeStruct((n_rep, rows, width), bf16),
         ),
-        in_specs=[SMEM_SPEC, SMEM_SPEC, VMEM_SPEC],
+        in_specs=[SMEM_SPEC, VMEM_SPEC],
         out_specs=(VMEM_SPEC, VMEM_SPEC),
-        scratch_shapes=[dma((7,)) for _ in range(4)],
+        scratch_shapes=[pltpu.VMEM((n_shard, rows, cols), bf16)]
+        + [dma((n_shard - 1,)) for _ in range(2)]
+        + [dma((10,)) for _ in range(4)],
         compiler_params=params(collective_id=2),
         name="share",
-    )(pick.reshape(1), keep.reshape(1), result)
-
-    update = pl.pallas_call(
-        functools.partial(update_kernel, update_scale),
-        out_shape=jax.ShapeDtypeStruct(momentum.shape, f32),
-        grid_spec=pltpu.PrefetchScalarGridSpec(
-            num_scalar_prefetch=1,
-            grid=(MATS,),
-            in_specs=[
-                pl.BlockSpec(
-                    (1, 2, 1, rows, cols), lambda q, p: (q // members, 0, q % members, 0, 0)
-                )
-            ],
-            out_specs=pl.BlockSpec((1, KV, cols), lambda q, p: (p[q], 0, 0)),
+    )(owner, result)
+
+    slot = jnp.arange(slots, dtype=i32)
+    momentum_out, update, owned = pl.pallas_call(
+        functools.partial(finish_kernel, update_scale),
+        out_shape=(
+            jax.ShapeDtypeStruct(momentum.shape, f32),
+            jax.ShapeDtypeStruct(momentum.shape, f32),
+            jax.ShapeDtypeStruct((slots, KV, width), bf16),
         ),
-        name="update",
-    )(perm, oall.reshape(groups, 2, members, rows, cols))
-
-    slot = jnp.arange(slots, dtype=i32)
-    owned = pl.pallas_call(
-        functools.partial(owned_kernel, update_scale),
-        out_shape=jax.ShapeDtypeStruct((slots, KV, width), bf16),
-        grid_spec=pltpu.PrefetchScalarGridSpec(
-            num_scalar_prefetch=2,
-            grid=(slots,),
-            in_specs=[pl.BlockSpec((1, 2, rows, width), lambda s, i, k: (i[s], 0, 0, 0))],
-            out_specs=pl.BlockSpec((1, KV, width), lambda s, i, k: (s, 0, 0)),
-        ),
-        name="owned",
+        in_specs=[SMEM_SPEC] * 5 + [VMEM_SPEC] * 3 + [ANY_SPEC],
+        out_specs=(ANY_SPEC,) * 3,
+        scratch_shapes=[
+            pltpu.VMEM(momentum.shape, f32),
+            pltpu.VMEM(momentum.shape, f32),
+            pltpu.VMEM((slots, KV, width), bf16),
+            dma((MATS,)), dma((MATS,)), dma((MATS,)), dma((slots,)),
+        ],
+        compiler_params=pltpu.CompilerParams(vmem_limit_bytes=VMEM_LIMIT),
+        name="finish",
     )(
-        (start + slot) % groups,
-        (slot < count).astype(f32),
-        whole.reshape(groups, 2, rows, width),
+        2 * (position // members), position % members, factors,
+        2 * ((start + slot) % groups), (slot < count).astype(f32),
+        gall, oall, whole, momentum,
     )
     return (momentum_out, update, owned)
 

time: 277 us -> 199 us (0.72)
  Pallas kernels: 265 us -> 184 us
  other arithmetic: 8.13 us -> 12.7 us
    pallas_call x4 -> x2, Pallas kernels: 49.3 us -> 20.6 us  [the longest x1 11.8 us: per_device_planes(): pl.pallas_call(functools.partial(finish_kernel, update_scale), out_shape=...]
    pallas_call x1, Pallas kernels: 43.2 us -> 20.4 us  [per_device_planes(): pl.pallas_call(functools.partial(spread_kernel, n_shard), out_shape=jax.S...]
    pallas_call x1, Pallas kernels: 122 us -> 103 us  [per_device_planes(): pl.pallas_call(functools.partial(reduce_kernel, n_shard, 1.0 / math.sqrt(...]
    pallas_call x1, Pallas kernels: 50.9 us -> 39.5 us  [per_device_planes(): pl.pallas_call(functools.partial(share_kernel, n_shard), out_shape=(jax.S...]
    reduce_sum x0 -> x3, other arithmetic: none -> 2.87 us  [the longest x1 1.41 us: per_device_planes(): jnp.sum(jnp.where(position[None, :] == member[:, None], owners[None, :],...]
where the time goes in v2:
time: 199 us; the launch traced here: 197 us
  Pallas kernels  184 us (92%)
  other arithmetic  12.7 us (6%)
    pallas_call x1, Pallas kernels, per_device_planes(): pl.pallas_call(functools.partial(reduce_kernel, n_shard, 1.0 / math.sqrt(...  103 us
    pallas_call x1, Pallas kernels, per_device_planes(): pl.pallas_call(functools.partial(share_kernel, n_shard), out_shape=(jax.S...  39.5 us
    pallas_call x1, Pallas kernels, per_device_planes(): pl.pallas_call(functools.partial(spread_kernel, n_shard), out_shape=jax.S...  20.4 us
    pallas_call x1, Pallas kernels, per_device_planes(): pl.pallas_call(functools.partial(finish_kernel, update_scale), out_shape=...  11.8 us
    pallas_call x1, Pallas kernels, per_device_planes(): pl.pallas_call(newton_kernel, out_shape=jax.ShapeDtypeStruct((KV, width),...  8.84 us

profile of v2, /device:TPU:17, one launch (start us, length us, event | category | flops | bytes accessed | tf_op | source)
XLA Modules:
  0.0 197.1 jit_solution(9540618548754878637)
XLA Ops:
  0.6 0.7 fusion.4
  1.4 0.9 convert_reduce_fusion
  2.3 0.8 convert_reduce_fusion.1
  3.1 0.6 broadcast_add_fusion
  3.7 0.6 and_select_fusion.5
  4.3 1.4 select_reduce_fusion.3.owner_ref
  5.7 0.7 select_reduce_fusion.2.mat_ref
  6.4 0.1 select_reduce_fusion.1
  6.5 0.5 fusion.13.block_ref
  7.0 0.5 and_select_fusion.3
  7.5 1.4 fusion.10
  8.9 1.2 compare_convert_fusion.1.keep_ref
  10.1 1.2 fusion.9.slot_ref
  11.3 103.0 %reduce.3 = (bf16[8,3,128,512]{3,2,1,0:T(8,128)(2,1)}, f32[4,8,3,1,512]{4,3,2,1,0:T(1,128)}) custom-call(s32[12]{0:T(128)} %get-tuple-element.20.lay_ref, s32[12]{0:T(128)} %get-tuple-element.19.half_ref, bf16[6,128,2048]{2,1,0:T(8,128)(2,1)} %act_ref.1, bf16[6,128,512]{2,1,0:T(8,128)(2,1)} %cot_ref.1), custom_call_target="tpu_custom_call" | custom-call | tf_op jit(solution)/shard_map/reduce/pallas_call | solution.py:541
  114.3 1.1 reduce_sum.118
  115.5 0.1 broadcast_in_dim.45
  115.6 0.2 select_reduce_fusion
  115.8 0.2 fusion.1
  116.0 0.5 multiply_minimum_fusion.factor_ref
  116.5 20.4 %spread.1.u_ref = bf16[256,2048]{1,0:T(8,128)(2,1)} custom-call(s32[4]{0:T(128)} %select_reduce_fusion.2.mat_ref, s32[4]{0:T(128)} %get-tuple-element.16.place_ref, f32[12]{0:T(128)} %multiply_minimum_fusion.factor_ref, f32[12,256,512]{2,1,0:T(8,128)} %momentum_ref.3, bf16[8,3,128,512]{3,2,1,0:T(8,128)(2,1)} %get-tuple-element.8.gall_ref), custom_call_target="tpu_custom_call" | custom-call | tf_op jit(solution)/shard_map/spread/pallas_call | solution.py:583
  136.9 8.8 %newton.1.o_ref = bf16[256,2048]{1,0:T(8,128)(2,1)} custom-call(bf16[256,2048]{1,0:T(8,128)(2,1)} %spread.1.u_ref), custom_call_target="tpu_custom_call" | custom-call | tf_op jit(solution)/shard_map/newton/pallas_call | solution.py:594
  145.8 39.5 %share.1 = (bf16[8,3,128,512]{3,2,1,0:T(8,128)(2,1)}, bf16[8,128,2048]{2,1,0:T(8,128)(2,1)}) custom-call(s32[3]{0:T(128)} %select_reduce_fusion.3.owner_ref, bf16[256,2048]{1,0:T(8,128)(2,1)} %newton.1.o_ref), custom_call_target="tpu_custom_call" | custom-call | tf_op jit(solution)/shard_map/share/pallas_call | solution.py:606
  185.3 11.8 %finish.1 = (f32[12,256,512]{2,1,0:T(8,128)}, f32[12,256,512]{2,1,0:T(8,128)}, bf16[4,256,2048]{2,1,0:T(8,128)(2,1)}) custom-call(s32[12]{0:T(128)} %fusion.13.block_ref, s32[12]{0:T(128)} %get-tuple-element.17.member_ref, f32[12]{0:T(128)} %multiply_minimum_fusion.factor_ref, s32[4]{0:T(128)} %fusion.9.slot_ref, f32[4]{0:T(128)} %compare_convert_fusion.1.keep_ref, ...), custom_call_target="tpu_custom_call" | custom-call | tf_op jit(solution)/shard_map/finish/pallas_call | solution.py:622
  (2 shorter events, 0.0 us)

commit v3 on v2

--- a/solution.py
+++ b/solution.py
@@ -197,8 +197,52 @@
     return at
 
 
+def plan_kernel(
+    n_shard, groups, owner_of, lay_ref, half_ref, position_ref, block_ref, member_ref,
+    mat_ref, place_ref, owner_ref, slot_ref, keep_ref, perm, sort,
+):
+    z = lax.axis_index("shard")
+    group = lax.div(lax.axis_index("rep"), 2)
+    members = owner_ref.shape[0]
+    owners = [owner_of[m] for m in range(MATS)]
+    one = lambda yes: yes.astype(jnp.int32)
+    for m in range(MATS):
+        rank = jnp.int32(0)
+        for j in range(MATS):
+            if j != m:
+                rank += one(owners[j] <= owners[m] if j < m else owners[j] < owners[m])
+        member = lax.div(rank, groups)
+        block = lax.rem(rank, groups)
+        position = block * members + member
+        position_ref[m] = position
+        block_ref[m] = 2 * block
+        member_ref[m] = member
+        lay_ref[position] = jnp.int32(m // 2)
+        half_ref[position] = jnp.int32(m % 2)
+        perm[position] = jnp.int32(m)
+        sort[position] = owners[m]
+    for j in range(members):
+        owner_ref[j] = sort[group * members + j]
+    for p in range(n_shard):
+        first = jnp.int32(0)
+        for m in range(MATS):
+            first += one(owners[m] < p)
+        skip = lax.rem(group + groups * MATS - first, groups)
+        place = lax.div(jnp.minimum(first + skip, MATS - 1), groups)
+        place_ref[p] = place
+        mat_ref[p] = perm[group * members + place]
+    start = jnp.int32(0)
+    count = jnp.int32(0)
+    for m in range(MATS):
+        start += one(owners[m] < z)
+        count += one(owners[m] == z)
+    for i in range(slot_ref.shape[0]):
+        slot_ref[i] = 2 * lax.rem(start + i, groups)
+        keep_ref[i] = one(count > i)
+
+
 def reduce_kernel(
-    n_shard, inverse, lay_ref, half_ref, act_ref, cot_ref, gall_ref, sq_ref,
+    n_shard, inverse, lay_ref, half_ref, act_ref, cot_ref, gown_ref, sq_ref,
     act, cot, part, recv1, turn, recv2, plane, zrecv,
     local_sem, in_send, in_recv, s1, r1, s2, r2, s3, r3, gs, gr, qs, qr,
 ):
@@ -208,7 +252,9 @@
     rows, cols = part.shape[-2:]
     members = part.shape[2 + 1]
     steps = [d for d in (2, 1, 3) if d < n_shard] + list(range(4, n_shard)) + [0]
-    peers = [(p, z) for p in (to_core, to_x, to_y, to_xy)]
+    other = 1 - 2 * core
+    near = (to_core, to_x, to_y, to_xy, to_x + other, to_y + other, to_xy + other)
+    peers = [(p, z) for p in near]
     peers += [(me, lax.rem(z + d, n_shard)) for d in range(1, n_shard)]
     own = [
         pltpu.make_async_copy(act_ref, act.at[:, pl.ds(0, tokens)], local_sem.at[0]),
@@ -319,43 +365,49 @@
         value = plane[n_shard - 1, j].astype(jnp.float32)
         for k in range(n_shard - 1):
             value = value + zrecv[k, j].astype(jnp.float32)
-        gall_ref[me, j] = (value * inverse).astype(gall_ref.dtype)
+        value = (value * inverse).astype(gown_ref.dtype)
+        gown_ref[core, j] = value
+        value = value.astype(jnp.float32)
+        line = jnp.sum(value * value, axis=0, keepdims=True)
+        lanes = sq_ref.shape[-1]
+        fold = line[:, :lanes]
+        for i in range(1, cols // lanes):
+            fold = fold + line[:, i * lanes : (i + 1) * lanes]
+        sq_ref[0, me, j] = fold
         return carry
 
     lax.fori_loop(0, members, add_last, 0)
-    at = block_at(gall_ref, 2)
-    copies = plane_gather_start(z, at, gs, gr)
-    plane_gather_turn(z, at, gs, gr, copies)
-    plane_gather_finish(z, at, gs, gr, copies)
-
-    def square(r, carry):
-        for j in range(members):
-            value = gall_ref[r, j].astype(jnp.float32)
-            sq_ref[0, r, j] = jnp.sum(value * value, axis=0, keepdims=True)
-        return carry
-
-    lax.fori_loop(0, gall_ref.shape[0], square, 0)
     fourth = []
+    for k, peer in enumerate(near):
+        c = remote(sq_ref.at[0, me], sq_ref.at[0, me], gs.at[k], gr.at[k], (peer, z))
+        c.start()
+        fourth.append(c)
+    c = remote(gown_ref.at[core], gown_ref.at[core], gs.at[len(near)], gr.at[len(near)], (to_core, z))
+    c.start()
+    for f in fourth:
+        f.wait_recv()
     for d in range(1, n_shard):
-        c = remote(
+        f = remote(
             sq_ref.at[0], sq_ref.at[d], qs.at[d - 1], qr.at[d - 1],
             (me, lax.rem(z + d, n_shard)),
         )
-        c.start()
-        fourth.append(c)
-    for c in fourth:
-        c.wait()
+        f.start()
+        fourth.append(f)
+    for f in fourth[len(near):]:
+        f.wait_recv()
+    c.wait_recv()
+    for f in fourth + [c]:
+        f.wait_send()
     for c in first + second + third:
         c.wait_send()
 
 
 def spread_kernel(
-    n_shard, mat_ref, place_ref, factor_ref, momentum_ref, gall_ref, full_ref,
-    held, zs, zr, cs, cr,
+    n_shard, mat_ref, place_ref, factor_ref, momentum_ref, gown_ref, full_ref, gall_ref,
+    held, zs, zr, cs, cr, gs, gr,
 ):
     me, core, x, y, to_core, to_x, to_y, to_xy = place()
     z = lax.axis_index("shard")
-    block = me - core
     rows = full_ref.shape[0] // 2
     cols = full_ref.shape[1] // n_shard
 
@@ -368,20 +420,26 @@
     def nesterov(p, side):
         matrix = mat_ref[p]
         half = pl.ds(pl.multiple_of(side * rows, rows), rows)
-        step = factor_ref[matrix] * gall_ref[block + side, place_ref[p]].astype(jnp.float32)
+        step = factor_ref[matrix] * gown_ref[side, place_ref[p]].astype(jnp.float32)
         new = momentum_rate * momentum_ref[matrix, half] + step
         return (step + momentum_rate * new).astype(full_ref.dtype)
 
     order = [d for d in (2, 1, 3) if d < n_shard] + list(range(4, n_shard))
     for d in order:
         held[d - 1] = nesterov(lax.rem(z + d, n_shard), core)
-    greet([(to_core, z)] + [(me, lax.rem(z + d, n_shard)) for d in range(1, n_shard)])
+    gall_ref[me] = gown_ref[core]
+    greet(
+        [(p, z) for p in (to_core, to_x, to_y)]
+        + [(me, lax.rem(z + d, n_shard)) for d in range(1, n_shard)]
+    )
     copies = []
     for d in order:
         peer = (me, lax.rem(z + d, n_shard))
         c = remote(held.at[d - 1], full_ref.at[at(core, z)], zs.at[d - 1], zr.at[d - 1], peer)
         c.start()
         copies.append(c)
+    at_g = block_at(gall_ref, 2)
+    gathers = plane_gather_start(z, at_g, gs, gr)
     for side in range(2):
         full_ref[at(side, z)] = nesterov(z, side)
     onward = []
@@ -391,8 +449,11 @@
         f = remote(source, source, cs.at[d - 1], cr.at[d - 1], (to_core, z))
         f.start()
         onward.append(f)
+        if len(onward) == 1:
+            plane_gather_turn(z, at_g, gs, gr, gathers)
     for f in onward:
         f.wait_recv()
+    plane_gather_finish(z, at_g, gs, gr, gathers)
     for c in copies + onward:
         c.wait_send()
 
@@ -484,7 +545,7 @@
     def owned_one(s):
         for c in range(2):
             value = scale * whole_ref[slot_ref[s] + c].astype(jnp.float32)
-            wbuf[s, pl.ds(c * rows, rows)] = (value * keep_ref[s]).astype(wbuf.dtype)
+            wbuf[s, pl.ds(c * rows, rows)] = (value * keep_ref[s].astype(jnp.float32)).astype(wbuf.dtype)
         put(wbuf, owned_ref, wsem, s).start()
 
     def update_one(m):
@@ -516,33 +577,32 @@
     token_total = tok_rows * n_shard * n_rep
     cols = width // n_shard
     rows = KV // 2
+    lanes = math.gcd(cols, 128)
     groups = n_rep // 2
     members = MATS // groups
     slots = -(-MATS // n_shard) + 1
     update_scale = math.sqrt(max(KV, D))
     bf16, f32, i32 = jnp.bfloat16, jnp.float32, jnp.int32
-    z = lax.axis_index("shard")
-    my_group = lax.axis_index("rep") // 2
-
+    shapes = [MATS] * 5 + [n_shard] * 2 + [members] + [slots] * 2
+    lay, half, position, block, member, mats, places, owner, slot_block, slot_keep = pl.pallas_call(
+        functools.partial(plan_kernel, n_shard, groups),
+        out_shape=[jax.ShapeDtypeStruct((n,), i32) for n in shapes],
+        in_specs=[SMEM_SPEC],
+        out_specs=[SMEM_SPEC] * len(shapes),
+        scratch_shapes=[pltpu.SMEM((MATS,), i32), pltpu.SMEM((MATS,), i32)],
+        name="plan",
+    )(owners)
     index = jnp.arange(MATS, dtype=i32)
-    before = (owners[None, :] < owners[:, None]) | (
-        (owners[None, :] == owners[:, None]) & (index[None, :] < index[:, None])
-    )
-    rank = jnp.sum(before.astype(i32), axis=1)
-    position = (rank % groups) * members + rank // groups
-    perm = jnp.sum(jnp.where(position[None, :] == index[:, None], index[None, :], 0), axis=1)
-    start = jnp.sum((owners < z).astype(i32))
-    count = jnp.sum((owners == z).astype(i32))
 
     params = functools.partial(
         pltpu.CompilerParams, has_side_effects=True, vmem_limit_bytes=VMEM_LIMIT
     )
     dma = pltpu.SemaphoreType.DMA
-    gall, sq = pl.pallas_call(
+    gown, sq = pl.pallas_call(
         functools.partial(reduce_kernel, n_shard, 1.0 / math.sqrt(token_total)),
         out_shape=(
-            jax.ShapeDtypeStruct((n_rep, members, rows, cols), bf16),
-            jax.ShapeDtypeStruct((n_shard, n_rep, members, 1, cols), f32),
+            jax.ShapeDtypeStruct((2, members, rows, cols), bf16),
+            jax.ShapeDtypeStruct((n_shard, n_rep, members, 1, lanes), f32),
         ),
         in_specs=[SMEM_SPEC, SMEM_SPEC, ANY_SPEC, ANY_SPEC],
         out_specs=(VMEM_SPEC, VMEM_SPEC),
@@ -558,38 +618,34 @@
             dma((2,)), dma((2,)), dma((2,)),
             dma((n_shard,)), dma((n_shard,)), dma((n_shard,)), dma((n_shard,)),
             dma((n_shard,)), dma((n_shard,)),
-            dma((10,)), dma((10,)), dma((n_shard - 1,)), dma((n_shard - 1,)),
+            dma((8,)), dma((8,)), dma((n_shard - 1,)), dma((n_shard - 1,)),
         ],
         compiler_params=params(collective_id=0),
         name="reduce",
-    )(perm // 2, perm % 2, activations, cotangents)
+    )(lay, half, activations, cotangents)
 
     by_position = jnp.sum(
-        sq.reshape(n_shard, groups, 2, members, cols), axis=(0, 2, 4)
+        sq.reshape(n_shard, groups, 2, members, lanes), axis=(0, 2, 4)
     ).reshape(MATS)
     square_sums = jnp.sum(
         jnp.where(position[:, None] == index[None, :], by_position[None, :], 0.0), axis=1
     )
     factors = clip_factors(square_sums, bucket_starts)
 
-    planes = jnp.arange(n_shard, dtype=i32)
-    firsts = jnp.sum((owners[None, :] < planes[:, None]).astype(i32), axis=1)
-    ranks = jnp.minimum(firsts + (my_group - firsts) % groups, MATS - 1)
-    places = ranks // groups
-    at_place = my_group * members + places
-    mats = jnp.sum(
-        jnp.where(position[None, :] == at_place[:, None], index[None, :], 0), axis=1
-    )
-    full = pl.pallas_call(
+    full, gall = pl.pallas_call(
         functools.partial(spread_kernel, n_shard),
-        out_shape=jax.ShapeDtypeStruct((KV, width), bf16),
+        out_shape=(
+            jax.ShapeDtypeStruct((KV, width), bf16),
+            jax.ShapeDtypeStruct((n_rep, members, rows, cols), bf16),
+        ),
         in_specs=[SMEM_SPEC, SMEM_SPEC, SMEM_SPEC, VMEM_SPEC, VMEM_SPEC],
-        out_specs=VMEM_SPEC,
+        out_specs=(VMEM_SPEC, VMEM_SPEC),
         scratch_shapes=[pltpu.VMEM((n_shard - 1, rows, cols), bf16)]
-        + [dma((n_shard - 1,)) for _ in range(4)],
+        + [dma((n_shard - 1,)) for _ in range(4)]
+        + [dma((10,)) for _ in range(2)],
         compiler_params=params(collective_id=1),
         name="spread",
-    )(mats, places, factors, momentum, gall)
+    )(mats, places, factors, momentum, gown)
 
     result = pl.pallas_call(
         newton_kernel,
@@ -599,10 +655,6 @@
         name="newton",
     )(full)
 
-    member = my_group * members + jnp.arange(members, dtype=i32)
-    owner = jnp.sum(
-        jnp.where(position[None, :] == member[:, None], owners[None, :], 0), axis=1
-    )
     oall, whole = pl.pallas_call(
         functools.partial(share_kernel, n_shard),
         out_shape=(
@@ -618,7 +670,6 @@
         name="share",
     )(owner, result)
 
-    slot = jnp.arange(slots, dtype=i32)
     momentum_out, update, owned = pl.pallas_call(
         functools.partial(finish_kernel, update_scale),
         out_shape=(
@@ -637,8 +688,7 @@
         compiler_params=pltpu.CompilerParams(vmem_limit_bytes=VMEM_LIMIT),
         name="finish",
     )(
-        2 * (position // members), position % members, factors,
-        2 * ((start + slot) % groups), (slot < count).astype(f32),
+        block, member, factors, slot_block, slot_keep,
         gall, oall, whole, momentum,
     )
     return (momentum_out, update, owned)

time: 199 us -> 181 us (0.910)
  other arithmetic: 12.7 us -> 3.25 us
  Pallas kernels: 184 us -> 175 us
    pallas_call x1, Pallas kernels: 103 us -> 87.9 us  [per_device_planes(): pl.pallas_call(functools.partial(reduce_kernel, n_shard, 1.0 / math.sqrt(...]
    reduce_sum x8 -> x2, other arithmetic: 6.44 us -> 0.96 us  [per_device_planes(): jnp.sum(sq.reshape(n_shard, groups, 2, members, lanes), axis=(0, 2, 4))]
    pallas_call x1 -> x2, Pallas kernels: 20.4 us -> 25.5 us  [the longest x1 24 us: per_device_planes(): pl.pallas_call(functools.partial(spread_kernel, n_shard), out_shape=(jax....]
where the time goes in v3:
time: 181 us; the launch traced here: 179 us
  Pallas kernels  175 us (97%)
  other arithmetic  3.25 us (2%)
    pallas_call x1, Pallas kernels, per_device_planes(): pl.pallas_call(functools.partial(reduce_kernel, n_shard, 1.0 / math.sqrt(...  87.9 us
    pallas_call x1, Pallas kernels, per_device_planes(): pl.pallas_call(functools.partial(share_kernel, n_shard), out_shape=(jax.S...  41.3 us
    pallas_call x1, Pallas kernels, per_device_planes(): pl.pallas_call(functools.partial(spread_kernel, n_shard), out_shape=(jax....  24 us
    pallas_call x1, Pallas kernels, per_device_planes(): pl.pallas_call(functools.partial(finish_kernel, update_scale), out_shape=...  11.8 us
    pallas_call x1, Pallas kernels, per_device_planes(): pl.pallas_call(newton_kernel, out_shape=jax.ShapeDtypeStruct((KV, width),...  8.84 us

profile of v3, /device:TPU:17, one launch (start us, length us, event | category | flops | bytes accessed | tf_op | source)
XLA Modules:
  0.0 179.4 jit_solution(7934730610819698956)
XLA Ops:
  0.6 0.7 fusion.2
  1.4 1.6 plan.1
  2.9 87.9 %reduce.3 = (bf16[2,3,128,512]{3,2,1,0:T(8,128)(2,1)}, f32[4,8,3,1,128]{4,3,2,1,0:T(1,128)}) custom-call(s32[12]{0:T(128)} %get-tuple-element.22.lay_ref, s32[12]{0:T(128)} %get-tuple-element.23.half_ref, bf16[6,128,2048]{2,1,0:T(8,128)(2,1)} %act_ref.1, bf16[6,128,512]{2,1,0:T(8,128)(2,1)} %cot_ref.1), custom_call_target="tpu_custom_call" | custom-call | tf_op jit(solution)/shard_map/reduce/pallas_call | solution.py:601
  90.9 0.9 reduce_sum.53
  91.8 0.1 broadcast_in_dim.14
  91.9 0.8 select_reduce_fusion
  92.7 0.2 fusion.1
  92.9 0.5 multiply_minimum_fusion.factor_ref
  93.5 24.0 %spread.1 = (bf16[256,2048]{1,0:T(8,128)(2,1)}, bf16[8,3,128,512]{3,2,1,0:T(8,128)(2,1)}) custom-call(s32[4]{0:T(128)} %get-tuple-element.27.mat_ref, s32[4]{0:T(128)} %get-tuple-element.28.place_ref, f32[12]{0:T(128)} %multiply_minimum_fusion.factor_ref, f32[12,256,512]{2,1,0:T(8,128)} %momentum_ref.3, bf16[2,3,128,512]{3,2,1,0:T(8,128)(2,1)} %get-tuple-element.29.gown_ref), custom_call_target="tpu_custom_call" | custom-call | tf_op jit(solution)/shard_map/spread/pallas_call | solution.py:635
  117.5 8.8 %newton.1.o_ref = bf16[256,2048]{1,0:T(8,128)(2,1)} custom-call(bf16[256,2048]{1,0:T(8,128)(2,1)} %get-tuple-element.32.u_ref), custom_call_target="tpu_custom_call" | custom-call | tf_op jit(solution)/shard_map/newton/pallas_call | solution.py:650
  126.3 41.3 %share.1 = (bf16[8,3,128,512]{3,2,1,0:T(8,128)(2,1)}, bf16[8,128,2048]{2,1,0:T(8,128)(2,1)}) custom-call(s32[3]{0:T(128)} %get-tuple-element.31.owner_ref, bf16[256,2048]{1,0:T(8,128)(2,1)} %newton.1.o_ref), custom_call_target="tpu_custom_call" | custom-call | tf_op jit(solution)/shard_map/share/pallas_call | solution.py:658
  167.6 11.8 %finish.1 = (f32[12,256,512]{2,1,0:T(8,128)}, f32[12,256,512]{2,1,0:T(8,128)}, bf16[4,256,2048]{2,1,0:T(8,128)(2,1)}) custom-call(s32[12]{0:T(128)} %get-tuple-element.19.block_ref, s32[12]{0:T(128)} %get-tuple-element.20.member_ref, f32[12]{0:T(128)} %multiply_minimum_fusion.factor_ref, s32[4]{0:T(128)} %get-tuple-element.25.slot_ref, ...), custom_call_target="tpu_custom_call" | custom-call | tf_op jit(solution)/shard_map/finish/pallas_call | solution.py:673
  (1 shorter events, 0.0 us)

commit v4 on v3

--- a/solution.py
+++ b/solution.py
@@ -256,29 +256,43 @@
     near = (to_core, to_x, to_y, to_xy, to_x + other, to_y + other, to_xy + other)
     peers = [(p, z) for p in near]
     peers += [(me, lax.rem(z + d, n_shard)) for d in range(1, n_shard)]
+    cut = [
+        pl.ds(pl.multiple_of(lax.rem(z + d, n_shard) * cols, cols), cols) for d in steps
+    ]
     own = [
-        pltpu.make_async_copy(act_ref, act.at[:, pl.ds(0, tokens)], local_sem.at[0]),
-        pltpu.make_async_copy(cot_ref, cot.at[:, pl.ds(0, tokens)], local_sem.at[1]),
+        pltpu.make_async_copy(
+            act_ref.at[:, :, cut[k]], act[k].at[:, pl.ds(0, tokens)], local_sem.at[k]
+        )
+        for k in range(n_shard)
     ]
+    own.append(
+        pltpu.make_async_copy(cot_ref, cot.at[:, pl.ds(0, tokens)], local_sem.at[n_shard])
+    )
     for c in own:
         c.start()
     greet(peers)
+    theirs = pl.ds(tokens, tokens)
     swap = [
-        remote(cot_ref, cot.at[:, pl.ds(tokens, tokens)], in_send.at[1], in_recv.at[1], (to_core, z)),
-        remote(act_ref, act.at[:, pl.ds(tokens, tokens)], in_send.at[0], in_recv.at[0], (to_core, z)),
+        remote(
+            act_ref.at[:, :, cut[k]], act[k].at[:, theirs],
+            in_send.at[k], in_recv.at[k], (to_core, z),
+        )
+        for k in range(n_shard)
     ]
-    for c in swap:
+    swap.append(
+        remote(cot_ref, cot.at[:, theirs], in_send.at[n_shard], in_recv.at[n_shard], (to_core, z))
+    )
+    for c in swap[-1:] + swap[:-1]:
         c.start()
     for c in own:
         c.wait()
-    for c in swap:
-        c.wait()
+    swap[n_shard].wait()
     first = []
     second = []
     third = []
 
     def launch(k):
-        offset = pl.multiple_of(lax.rem(z + steps[k], n_shard) * cols, cols)
+        swap[k].wait()
 
         def one(q, carry):
             group = lax.div(q, members)
@@ -287,7 +301,7 @@
             low = jnp.where(core == 0, block[:, :rows], block[:, rows : 2 * rows])
             high = jnp.where(core == 0, block[:, 2 * rows : 3 * rows], block[:, 3 * rows :])
             left = jnp.where(half_ref[q] == 0, low, high)
-            right = act[lay_ref[q], :, pl.ds(offset, cols)]
+            right = act[k][lay_ref[q]]
             value = lax.dot_general(
                 left, right, (((0,), (0,)), ((), ())), preferred_element_type=jnp.float32
             )
@@ -607,7 +621,7 @@
         in_specs=[SMEM_SPEC, SMEM_SPEC, ANY_SPEC, ANY_SPEC],
         out_specs=(VMEM_SPEC, VMEM_SPEC),
         scratch_shapes=[
-            pltpu.VMEM((layers, 2 * tok_rows, width), bf16),
+            [pltpu.VMEM((layers, 2 * tok_rows, cols), bf16) for _ in range(n_shard)],
             pltpu.VMEM((layers, 2 * tok_rows, 2 * KV), bf16),
             pltpu.VMEM((n_shard, 2, 2, members, rows, cols), bf16),
             pltpu.VMEM((n_shard, 2, members, rows, cols), bf16),
@@ -615,7 +629,7 @@
             pltpu.VMEM((n_shard, members, rows, cols), bf16),
             pltpu.VMEM((n_shard, members, rows, cols), bf16),
             pltpu.VMEM((n_shard - 1, members, rows, cols), bf16),
-            dma((2,)), dma((2,)), dma((2,)),
+            dma((n_shard + 1,)), dma((n_shard + 1,)), dma((n_shard + 1,)),
             dma((n_shard,)), dma((n_shard,)), dma((n_shard,)), dma((n_shard,)),
             dma((n_shard,)), dma((n_shard,)),
             dma((8,)), dma((8,)), dma((n_shard - 1,)), dma((n_shard - 1,)),

time: 181 us -> 178 us (0.983)
  Pallas kernels: 175 us -> 172 us
    pallas_call x1, Pallas kernels: 87.9 us -> 84.6 us  [per_device_planes(): pl.pallas_call(functools.partial(reduce_kernel, n_shard, 1.0 / math.sqrt(...]
where the time goes in v4:
time: 178 us; the launch traced here: 176 us
  Pallas kernels  172 us (97%)
  other arithmetic  3.25 us (2%)
    pallas_call x1, Pallas kernels, per_device_planes(): pl.pallas_call(functools.partial(reduce_kernel, n_shard, 1.0 / math.sqrt(...  84.6 us
    pallas_call x1, Pallas kernels, per_device_planes(): pl.pallas_call(functools.partial(share_kernel, n_shard), out_shape=(jax.S...  41.3 us
    pallas_call x1, Pallas kernels, per_device_planes(): pl.pallas_call(functools.partial(spread_kernel, n_shard), out_shape=(jax....  24 us
    pallas_call x1, Pallas kernels, per_device_planes(): pl.pallas_call(functools.partial(finish_kernel, update_scale), out_shape=...  11.8 us
    pallas_call x1, Pallas kernels, per_device_planes(): pl.pallas_call(newton_kernel, out_shape=jax.ShapeDtypeStruct((KV, width),...  8.83 us

profile of v4, /device:TPU:17, one launch (start us, length us, event | category | flops | bytes accessed | tf_op | source)
XLA Modules:
  0.0 176.2 jit_solution(3249654782986654238)
XLA Ops:
  0.6 0.7 fusion.2
  1.4 1.6 plan.1
  2.9 84.6 %reduce.3 = (bf16[2,3,128,512]{3,2,1,0:T(8,128)(2,1)}, f32[4,8,3,1,128]{4,3,2,1,0:T(1,128)}) custom-call(s32[12]{0:T(128)} %get-tuple-element.22.lay_ref, s32[12]{0:T(128)} %get-tuple-element.23.half_ref, bf16[6,128,2048]{2,1,0:T(8,128)(2,1)} %act_ref.1, bf16[6,128,512]{2,1,0:T(8,128)(2,1)} %cot_ref.1), custom_call_target="tpu_custom_call" | custom-call | tf_op jit(solution)/shard_map/reduce/pallas_call | solution.py:615
  87.6 0.9 reduce_sum.53
  88.5 0.1 broadcast_in_dim.14
  88.6 0.8 select_reduce_fusion
  89.5 0.2 fusion.1
  89.7 0.5 multiply_minimum_fusion.factor_ref
  90.2 24.0 %spread.1 = (bf16[256,2048]{1,0:T(8,128)(2,1)}, bf16[8,3,128,512]{3,2,1,0:T(8,128)(2,1)}) custom-call(s32[4]{0:T(128)} %get-tuple-element.27.mat_ref, s32[4]{0:T(128)} %get-tuple-element.28.place_ref, f32[12]{0:T(128)} %multiply_minimum_fusion.factor_ref, f32[12,256,512]{2,1,0:T(8,128)} %momentum_ref.3, bf16[2,3,128,512]{3,2,1,0:T(8,128)(2,1)} %get-tuple-element.29.gown_ref), custom_call_target="tpu_custom_call" | custom-call | tf_op jit(solution)/shard_map/spread/pallas_call | solution.py:649
  114.2 8.8 %newton.1.o_ref = bf16[256,2048]{1,0:T(8,128)(2,1)} custom-call(bf16[256,2048]{1,0:T(8,128)(2,1)} %get-tuple-element.32.u_ref), custom_call_target="tpu_custom_call" | custom-call | tf_op jit(solution)/shard_map/newton/pallas_call | solution.py:664
  123.0 41.3 %share.1 = (bf16[8,3,128,512]{3,2,1,0:T(8,128)(2,1)}, bf16[8,128,2048]{2,1,0:T(8,128)(2,1)}) custom-call(s32[3]{0:T(128)} %get-tuple-element.31.owner_ref, bf16[256,2048]{1,0:T(8,128)(2,1)} %newton.1.o_ref), custom_call_target="tpu_custom_call" | custom-call | tf_op jit(solution)/shard_map/share/pallas_call | solution.py:672
  164.4 11.8 %finish.1 = (f32[12,256,512]{2,1,0:T(8,128)}, f32[12,256,512]{2,1,0:T(8,128)}, bf16[4,256,2048]{2,1,0:T(8,128)(2,1)}) custom-call(s32[12]{0:T(128)} %get-tuple-element.19.block_ref, s32[12]{0:T(128)} %get-tuple-element.20.member_ref, f32[12]{0:T(128)} %multiply_minimum_fusion.factor_ref, s32[4]{0:T(128)} %get-tuple-element.25.slot_ref, ...), custom_call_target="tpu_custom_call" | custom-call | tf_op jit(solution)/shard_map/finish/pallas_call | solution.py:687
  (1 shorter events, 0.0 us)
